TPU v7x, 256 devices: a 2x2x32 block of a 4x8x32 slice. The times are simulated.
256 devices in a mesh: groups: 4 (over y, x), seq: 32 (over z), head: 2 (over core).
Axes of the slice: x: 2, y: 2, z: 32, core: 2. Of those that a mesh axis runs over, the one named last changes fastest.
The devices are a block of a 4x8x32 slice.
Arguments:
- q_latent: bfloat16 [128, 64, 512], P(('groups', 'seq'), 'head'), parts along dimension 0, may hold values from -7.5 to 7.5
- q_rope: bfloat16 [128, 4096], P(('groups', 'seq'), 'head'), parts along dimension 0, may hold values from -7.5 to 7.5
- cache_latent: bfloat16 [24576, 64, 512], P(('groups', 'seq', 'head')), parts along dimension 0, may hold values from -10 to 10
- cache_rope: bfloat16 [24576, 4096], P(('groups', 'seq', 'head')), parts along dimension 0, may hold values from -6 to 6
- page_table: int32 [128, 192], P('groups'), parts along dimension 0, may hold values from 0 to 6143, as said below
- lengths: int32 [128], P('groups'), parts along dimension 0, may hold values from 1 to 12288, 235929 in all
Outputs:
- attended: bfloat16 [128, 64, 512], P(('groups', 'seq'), 'head'), parts along dimension 0
There are 4 independent parts, one for each index of `groups`. A program takes and returns all parts, laid end to end along the dimension named above; each array names one. Nothing has to cross between parts.
Inputs may be any that keep to these rules, and one draw needn't show every extreme that they name: `page_table`: device d of a group (d = seq index * 2 + head index) holds pool pages d * 96 to (d + 1) * 96 - 1. Each pool page is named exactly once. A request's logical pages k * 3 to (k + 1) * 3 - 1 lie on one device, and every device holds exactly one such run of every request. `lengths`: the newest token is counted.
All inputs are finite; a program needn't handle non-finite values.
Results may differ from a plain program's by a relative error of at most 0.0055.
Values may be sent and summed in bfloat16 or wider, within the bound.
No kernel may reach another device: no remote copies, remote signals or barrier semaphores. Data moves between devices by JAX's collectives and lax.ppermute only.
A program may use at most 128 MiB of HBM per device.

v0:
```python
import math

import jax
import jax.numpy as jnp
from jax import lax
from jax.experimental import pallas as pl
from jax.experimental.pallas import tpu as pltpu
from jax.sharding import PartitionSpec as P


ROPE = 64
NOPE = 128
LANES = 128
STAT_ROWS = 16
MASKED_SCORE = -1e30

FAR = (0, 6, 13, -6, -13)
NEAR = {
    1: FAR,
    -1: FAR,
    2: FAR,
    -2: FAR,
    3: (0, 6, 13, -13),
    -3: (0, 13, -6),
}
GROUPS = ((0, FAR),) + tuple(NEAR.items())

VMEM = pl.BlockSpec(memory_space=pltpu.VMEM)
HBM = pl.BlockSpec(memory_space=pltpu.HBM)
LIMIT = pltpu.CompilerParams(vmem_limit_bytes=12 << 20)


def shift_from(array, offset):
    count, cores = lax.axis_size("seq"), lax.axis_size("head")
    pairs = [
        (((i + (1 - 2 * c) * offset) % count) * cores + c, i * cores + c)
        for i in range(count)
        for c in range(cores)
    ]
    return lax.ppermute(array, ("seq", "head"), pairs)


def swapped(array):
    cores = lax.axis_size("head")
    return lax.ppermute(array, "head", [(c, cores - 1 - c) for c in range(cores)])


def joined(arrays, *picks):
    def kernel(*refs):
        for out_ref, pick in zip(refs[len(arrays) :], picks):
            for at, (k, i) in enumerate(pick):
                out_ref[at] = refs[k][i]

    shape = arrays[0].shape[1:]
    outs = pl.pallas_call(
        kernel,
        out_shape=[jax.ShapeDtypeStruct((len(p),) + shape, arrays[0].dtype) for p in picks],
        in_specs=[VMEM] * len(arrays),
        out_specs=[VMEM] * len(picks),
        compiler_params=LIMIT,
    )(*arrays)
    return outs[0] if len(picks) == 1 else outs


def parts_of(x, count):
    parts = []
    for _ in range(count - 1):
        high = x.astype(jnp.bfloat16).astype(jnp.float32)
        parts.append(high)
        x = x - high
    return parts + [x]


def pack_kernel(q_ref, rope_ref, out_ref):
    heads, width = q_ref.shape[1:]
    for c in range(width // LANES):
        out_ref[0, c * heads : (c + 1) * heads, :] = q_ref[0, :, c * LANES : (c + 1) * LANES]
    out_ref[0, heads * width // LANES :, :] = rope_ref[...]


def request_at(table_ref, offset, count):
    return lax.rem(table_ref[0] + table_ref[1] * offset + count, count)


def gather_kernel(run_len, count, table_ref, own_lat, partner_lat, own_rot, partner_rot, *refs):
    outs, sems = refs[:-1], refs[-1]
    entry = 2 * (run_len + 1)
    for k, (d, held) in enumerate(GROUPS):
        keys_ref, rotary_ref = outs[2 * k], outs[2 * k + 1]
        for g, o in enumerate(held):
            request = request_at(table_ref, o + d, count)
            for which, (lat, rot) in enumerate(((own_lat, own_rot), (partner_lat, partner_rot))):
                for j in range(run_len):
                    page = table_ref[2 + request * entry + which * (run_len + 1) + j]
                    slot = which * run_len + j
                    for kind, (cache, to_ref) in enumerate(((lat, keys_ref), (rot, rotary_ref))):
                        size = cache.shape[1]
                        pltpu.make_async_copy(
                            cache.at[page], to_ref.at[g, pl.ds(slot * size, size)], sems.at[2 * k + kind]
                        ).start()
    for k, ref in enumerate(outs):
        pltpu.make_async_copy(ref, ref, sems.at[k]).wait()


def gather_pages(table, caches, run_len, count):
    shapes = []
    for _, held in GROUPS:
        for cache in caches[::2]:
            size, lanes = cache.shape[1:]
            shapes.append(jax.ShapeDtypeStruct((len(held), 2 * run_len * size, lanes), jnp.bfloat16))
    outs = pl.pallas_call(
        lambda *refs: gather_kernel(run_len, count, *refs),
        out_shape=shapes,
        in_specs=[pl.BlockSpec(memory_space=pltpu.SMEM)] + [HBM] * 4,
        out_specs=[VMEM] * len(shapes),
        scratch_shapes=[pltpu.SemaphoreType.DMA((len(shapes),))],
        compiler_params=pltpu.CompilerParams(vmem_limit_bytes=34 << 20),
        cost_estimate=pl.CostEstimate(
            flops=1 << 32, bytes_accessed=2 * sum(s.size * 2 for s in shapes), transcendentals=0
        ),
        name="gather_pages",
    )(table, *caches)
    return [(outs[2 * k], outs[2 * k + 1]) for k in range(len(GROUPS))]


def attention_kernel(offsets, run_len, count, table_ref, q_ref, keys_ref, rotary_ref, out_ref):
    tokens, width = keys_ref.shape[1:]
    packed = q_ref.shape[1] - STAT_ROWS
    slabs = width // LANES
    heads = packed // slabs
    half = tokens // 2
    entry = 2 * (run_len + 1)
    lane = lax.broadcasted_iota(jnp.int32, (heads, LANES), 1)
    rope_lane = lax.broadcasted_iota(jnp.int32, (STAT_ROWS, LANES), 1)
    column = lax.broadcasted_iota(jnp.int32, (heads, tokens), 1)
    row_of = lax.broadcasted_iota(jnp.int32, (tokens, tokens // 2), 0) // 2
    row_in = lax.broadcasted_iota(jnp.int32, (tokens, tokens // 2), 1)
    spread = jnp.where(row_of == row_in, 1.0, 0.0).astype(jnp.bfloat16)
    token_odd = lax.broadcasted_iota(jnp.int32, (tokens, LANES), 0) % 2
    half_of = lax.broadcasted_iota(jnp.int32, (tokens, LANES), 1) // ROPE
    kept = token_odd == half_of
    over_width = (((1,), (1,)), ((), ()))
    each = range(len(offsets))
    scores, lives = [], []
    for g in each:
        query = jnp.concatenate(
            [q_ref[g, c * heads : (c + 1) * heads, :] for c in range(slabs)], axis=1
        )
        rope = q_ref[g, packed:, :].astype(jnp.float32)
        other = pltpu.roll(rope, ROPE, 1)
        query_rope = jnp.concatenate(
            [jnp.where(rope_lane < ROPE, rope, other), jnp.where(rope_lane < ROPE, other, rope)],
            axis=0,
        ).astype(jnp.bfloat16)
        rotary = jnp.dot(spread, rotary_ref[g], preferred_element_type=jnp.float32)
        rotary = jnp.where(kept, rotary, 0.0).astype(jnp.bfloat16)
        score = lax.dot_general(query, keys_ref[g], over_width, preferred_element_type=jnp.float32)
        score = score + lax.dot_general(
            query_rope, rotary, over_width, preferred_element_type=jnp.float32
        )
        request = request_at(table_ref, offsets[g], count)
        own_live = table_ref[2 + request * entry + run_len]
        partner_live = table_ref[2 + request * entry + 2 * run_len + 1]
        live = column < jnp.where(column < half, own_live, half + partner_live)
        lives.append(live)
        scores.append(jnp.where(live, score * (1.0 / math.sqrt(NOPE + ROPE)), MASKED_SCORE))
    tops = [jnp.max(score, axis=1, keepdims=True) for score in scores]
    probs = [jnp.where(lives[g], jnp.exp(scores[g] - tops[g]), 0.0) for g in each]
    totals = [jnp.sum(prob, axis=1, keepdims=True) for prob in probs]
    for g in each:
        summed = jnp.dot(
            probs[g].astype(jnp.bfloat16), keys_ref[g], preferred_element_type=jnp.float32
        ).astype(jnp.bfloat16)
        for c in range(slabs):
            out_ref[g, c * heads : (c + 1) * heads, :] = summed[:, c * LANES : (c + 1) * LANES]
    for g in each:
        stats = jnp.zeros((heads, LANES), jnp.float32)
        for i, part in enumerate(parts_of(tops[g], 3) + parts_of(totals[g], 2)):
            stats = jnp.where(lane == i, part, stats)
        out_ref[g, packed:, :] = jnp.zeros((STAT_ROWS, LANES), out_ref.dtype)
        out_ref[g, packed:, :heads] = stats.T[:STAT_ROWS].astype(out_ref.dtype)


def attention(offsets, table, queries, pages, run_len, count):
    groups, rows, _ = queries.shape
    tokens, width = pages[0].shape[1:]
    heads = (rows - STAT_ROWS) * LANES // width
    work = groups * tokens
    return pl.pallas_call(
        lambda *refs: attention_kernel(offsets, run_len, count, *refs),
        out_shape=jax.ShapeDtypeStruct((groups, rows, LANES), jnp.bfloat16),
        in_specs=[pl.BlockSpec(memory_space=pltpu.SMEM)] + [VMEM] * 3,
        out_specs=VMEM,
        compiler_params=LIMIT,
        cost_estimate=pl.CostEstimate(
            flops=work * heads * (4 * width + 4 * ROPE),
            bytes_accessed=work * (width + LANES) * 2,
            transcendentals=work * heads,
        ),
        name="attention",
    )(table, queries, *pages)


def merge_blocks(blocks, packed, heads, final):
    rows = [ref[i, packed:, :].astype(jnp.float32) for ref, i in blocks]
    tops = [r[0:1] + r[1:2] + r[2:3] for r in rows]
    totals = [r[3:4] + r[4:5] for r in rows]
    best = tops[0]
    for top in tops[1:]:
        best = jnp.maximum(best, top)
    weights = [jnp.exp(top - best) for top in tops]
    total = sum(w * t for w, t in zip(weights, totals))
    if final:
        weights = [w / total for w in weights]
    padded = weights + [jnp.zeros_like(best)] * (8 - len(weights))
    columns = jnp.concatenate(padded, axis=0).T
    columns = [columns[:heads, k : k + 1] for k in range(len(blocks))]
    slabs = []
    for c in range(packed // heads):
        slab = 0.0
        for column, (ref, i) in zip(columns, blocks):
            slab += column * ref[i, c * heads : (c + 1) * heads, :].astype(jnp.float32)
        slabs.append(slab.astype(jnp.bfloat16))
    if final:
        return slabs, None
    stats = parts_of(best, 3) + parts_of(total, 2)
    stats += [jnp.zeros((STAT_ROWS - len(stats), LANES), jnp.float32)]
    return slabs, jnp.concatenate(stats, axis=0).astype(jnp.bfloat16)


def near_merge_kernel(heads, sources, *refs):
    inputs, outs = refs[: len(sources)], refs[len(sources) :]
    packed = outs[0].shape[1] - STAT_ROWS
    places = ((0, 0), (1, 0), (1, 1), (2, 0), (2, 1))
    for o, (k, i) in zip(FAR, places):
        blocks = [(ref, held.index(o)) for ref, held in zip(inputs, sources) if o in held]
        slabs, stats = merge_blocks(blocks, packed, heads, False)
        for c, slab in enumerate(slabs):
            outs[k][i, c * heads : (c + 1) * heads, :] = slab
        outs[k][i, packed:, :] = stats


def far_merge_kernel(blocks, *refs):
    inputs, out_ref = refs[:-1], refs[-1]
    heads = out_ref.shape[1]
    packed = inputs[0].shape[1] - STAT_ROWS
    slabs, _ = merge_blocks([(inputs[k], i) for k, i in blocks], packed, heads, True)
    for c, slab in enumerate(slabs):
        out_ref[0, :, c * LANES : (c + 1) * LANES] = slab


def local(q_latent, q_rope, cache_latent, cache_rope, page_table, lengths):
    seq_count = lax.axis_size("seq")
    head_count = lax.axis_size("head")
    my_seq = lax.axis_index("seq")
    my_core = lax.axis_index("head")
    pool_pages, page_len, latent_width = cache_latent.shape
    rope_width = cache_rope.shape[1] // page_len
    request_count, page_slots = page_table.shape
    device_count = seq_count * head_count
    run_len = page_slots // device_count
    heads = q_latent.shape[1]
    reached = [(o + d) % seq_count for d, held in GROUPS for o in held]
    assert sorted(reached) == list(range(seq_count)) and head_count == 2

    rope_rows = q_rope.reshape(2, heads // 2, rope_width)
    rope_rows = jnp.concatenate([rope_rows[0], rope_rows[1]], axis=1)
    block_shape = (1, heads * latent_width // LANES + STAT_ROWS, LANES)
    block = pl.pallas_call(
        pack_kernel,
        out_shape=jax.ShapeDtypeStruct(block_shape, jnp.bfloat16),
        in_specs=[VMEM] * 2,
        out_specs=VMEM,
        compiler_params=LIMIT,
        name="pack",
    )(q_latent, rope_rows)

    other = swapped(block)
    pair = joined([block, other], ((0, 0), (1, 0)))
    thirteen = shift_from(pair, FAR[2])
    six = shift_from(pair, FAR[1])

    lat_sent, rope_sent, _ = lax.optimization_barrier((cache_latent, cache_rope, pair))
    partner_lat, partner_rope = swapped(lat_sent), swapped(rope_sent)
    own_rope, partner_rope, table_read = lax.optimization_barrier(
        (cache_rope, partner_rope, page_table)
    )

    rows = page_len * rope_width // LANES
    own_rot, partner_rot = (
        rope.reshape(pool_pages, rows, LANES) for rope in (own_rope, partner_rope)
    )
    caches = (cache_latent, partner_lat, own_rot, partner_rot)

    run_owner = table_read[:, ::run_len] // pool_pages
    run_ids = jnp.arange(device_count, dtype=jnp.int32)
    slots = table_read.reshape(request_count, device_count, run_len)

    def runs_on(device):
        here = run_owner == device
        run_index = jnp.sum(jnp.where(here, run_ids[None, :], 0), axis=1)
        pages = jnp.sum(jnp.where(here[:, :, None], slots, 0), axis=1) - device * pool_pages
        live = jnp.clip(lengths - run_index * run_len * page_len, 0, run_len * page_len)
        return [pages, live[:, None]]

    entries = runs_on(my_seq * head_count + my_core)
    entries += runs_on(my_seq * head_count + head_count - 1 - my_core)
    table = jnp.concatenate(entries, axis=1).astype(jnp.int32).reshape(-1)
    place = jnp.stack([my_seq, 1 - 2 * my_core]).astype(jnp.int32)
    table = jnp.concatenate([place, table])
    pages = gather_pages(table, caches, run_len, seq_count)

    six, thirteen, _ = lax.optimization_barrier((six, thirteen, pages[-1][1]))
    crossing = swapped(joined([six, thirteen], ((0, 1), (1, 1))))
    where = {0: (0, 0), 6: (1, 0), 13: (2, 0), -6: (3, 0), -13: (3, 1)}
    lists = [held for held in dict.fromkeys(held for _, held in GROUPS)]
    fars = joined([block, six, thirteen, crossing], *[[where[o] for o in held] for held in lists])
    fars = dict(zip(lists, fars))

    near = {d: shift_from(fars[held], d) for d, held in NEAR.items()}
    partials, sources = [], []
    for (d, held), group_pages in zip(GROUPS, pages):
        offsets = tuple(o + d for o in held)
        queries = near[d] if d else fars[held]
        partial = attention(offsets, table, queries, group_pages, run_len, seq_count)
        partials.append(shift_from(partial, -d) if d else partial)
        sources.append(held)

    home, ahead, across = pl.pallas_call(
        lambda *refs: near_merge_kernel(heads, sources, *refs),
        out_shape=[jax.ShapeDtypeStruct((n,) + block_shape[1:], jnp.bfloat16) for n in (1, 2, 2)],
        in_specs=[VMEM] * len(sources),
        out_specs=[VMEM] * 3,
        compiler_params=LIMIT,
        name="near_merge",
    )(*partials)
    taken = swapped(across)
    pair_six, pair_thirteen = joined([ahead, taken], ((0, 0), (1, 0)), ((0, 1), (1, 1)))
    thirteen = shift_from(pair_thirteen, -FAR[2])
    six = shift_from(pair_six, -FAR[1])
    crossing = swapped(joined([six, thirteen], ((0, 1), (1, 1))))
    arrived = [home, six, thirteen, crossing]
    blocks = ((0, 0), (1, 0), (2, 0), (3, 0), (3, 1))
    return pl.pallas_call(
        lambda *refs: far_merge_kernel(blocks, *refs),
        out_shape=jax.ShapeDtypeStruct((1, heads, latent_width), jnp.bfloat16),
        in_specs=[VMEM] * len(arrived),
        out_specs=VMEM,
        compiler_params=LIMIT,
        name="far_merge",
    )(*arrived)


def solution(mesh):
    return jax.shard_map(
        local,
        mesh=mesh,
        in_specs=(
            P(("groups", "seq"), "head", None),
            P(("groups", "seq"), "head"),
            P(("groups", "seq", "head"), None, None),
            P(("groups", "seq", "head"), None),
            P("groups", None),
            P("groups"),
        ),
        out_specs=P(("groups", "seq"), "head", None),
        check_vma=False,
    )
```

profile of v0, /device:TPU:38, one launch (start us, length us, event | category | flops | bytes accessed | tf_op | source)
XLA Modules:
  0.0 136.3 jit_solution(6269626412153801159)
XLA Ops:
  3.5 25.5 %collective-permute-start.2 = (bf16[2,144,128]{2,1,0:T(8,128)(2,1)S(1)}, bf16[2,144,128]{2,1,0:T(8,128)(2,1)S(1)}, u32[]{:S(2)}, u32[]{:S(2)}) collective-permute-start(bf16[2,144,128]{2,1,0:T(8,128)(2,1)S(1)} %shard_map.64), channel_id=1, source_target_pairs={{12,0},{53,1},{14,2},{55,3},{16,4},{57,5},{18,6},{59,7},{20,8},{61... | collective-permute-start | bytes 221192 | tf_op jit(solution)/shard_map/ppermute | solution.py:40
  28.9 4.1 %collective-permute-start.3 = (bf16[2,144,128]{2,1,0:T(8,128)(2,1)S(1)}, bf16[2,144,128]{2,1,0:T(8,128)(2,1)S(1)}, u32[]{:S(2)}, u32[]{:S(2)}) collective-permute-start(bf16[2,144,128]{2,1,0:T(8,128)(2,1)S(1)} %shard_map.64), channel_id=1, source_target_pairs={{26,0},{39,1},{28,2},{41,3},{30,4},{43,5},{32,6},{45,7},{34,8},{47... | collective-permute-start | bytes 221192 | tf_op jit(solution)/shard_map/ppermute | solution.py:40
  36.4 1.3 copy.18
  37.9 5.6 %gather_pages.1 = (bf16[5,384,512]{2,1,0:T(8,128)(2,1)S(1)}, bf16[5,192,128]{2,1,0:T(8,128)(2,1)S(1)}, bf16[5,384,512]{2,1,0:T(8,128)(2,1)S(1)}, bf16[5,192,128]...) custom-call(s32[258]{0:T(512)S(1)} %pad_add_fusion.1.refs_0_, ...), custom_call_target="tpu_custom_call" | custom-call | flops 4294967296 | bytes 28311552 | tf_op jit(solution)/shard_map/gather_pages/pallas_call | solution.py:111
  43.5 8.5 %collective-permute-done.3.refs_1_.refs_2_ = bf16[2,144,128]{2,1,0:T(8,128)(2,1)S(1)} collective-permute-done((bf16[2,144,128]{2,1,0:T(8,128)(2,1)S(1)}, bf16[2,144,128]{2,1,0:T(8,128)(2,1)S(1)}, u32[]{:S(2)}, u32[]{:S(2)}) %collective-permute-start.3) | collective-permute-done | bytes 73760 | tf_op jit(solution)/shard_map/ppermute | solution.py:40
  53.4 2.4 %collective-permute-start.16 = (bf16[3,144,128]{2,1,0:T(8,128)(2,1)S(1)}, bf16[3,144,128]{2,1,0:T(8,128)(2,1)S(1)}, u32[]{:S(2)}, u32[]{:S(2)}) collective-permute-start(bf16[3,144,128]{2,1,0:T(8,128)(2,1)S(1)} %get-tuple-element.56), channel_id=1, source_target_pairs={{58,0},{7,1},{60,2},{9,3},{62,4},{11,5},{0,6},{13,7},{2,8},{15,9},... | collective-permute-start | bytes 331784 | tf_op jit(solution)/shard_map/ppermute | solution.py:40
  55.8 1.9 %collective-permute-start.10 = (bf16[5,144,128]{2,1,0:T(8,128)(2,1)S(1)}, bf16[5,144,128]{2,1,0:T(8,128)(2,1)S(1)}, u32[]{:S(2)}, u32[]{:S(2)}) collective-permute-start(bf16[5,144,128]{2,1,0:T(8,128)(2,1)S(1)} %get-tuple-element.42.refs_1_), channel_id=1, source_target_pairs={{4,0},{61,1},{6,2},{63,3},{8,4},{1,5},{10,6},{3,7},{12,8},{5,9},{1... | collective-permute-start | bytes 552968 | tf_op jit(solution)/shard_map/ppermute | solution.py:40
  57.7 2.9 %collective-permute-start.8 = (bf16[5,144,128]{2,1,0:T(8,128)(2,1)S(1)}, bf16[5,144,128]{2,1,0:T(8,128)(2,1)S(1)}, u32[]{:S(2)}, u32[]{:S(2)}) collective-permute-start(bf16[5,144,128]{2,1,0:T(8,128)(2,1)S(1)} %get-tuple-element.42.refs_1_), channel_id=1, source_target_pairs={{62,0},{3,1},{0,2},{5,3},{2,4},{7,5},{4,6},{9,7},{6,8},{11,9},{8,1... | collective-permute-start | bytes 552968 | tf_op jit(solution)/shard_map/ppermute | solution.py:40
  60.9 4.4 %collective-permute-done.16.refs_1_ = bf16[3,144,128]{2,1,0:T(8,128)(2,1)S(1)} collective-permute-done((bf16[3,144,128]{2,1,0:T(8,128)(2,1)S(1)}, bf16[3,144,128]{2,1,0:T(8,128)(2,1)S(1)}, u32[]{:S(2)}, u32[]{:S(2)}) %collective-permute-start.16) | collective-permute-done | bytes 110624 | tf_op jit(solution)/shard_map/ppermute | solution.py:40
  65.3 2.9 %collective-permute-start.14 = (bf16[4,144,128]{2,1,0:T(8,128)(2,1)S(1)}, bf16[4,144,128]{2,1,0:T(8,128)(2,1)S(1)}, u32[]{:S(2)}, u32[]{:S(2)}) collective-permute-start(bf16[4,144,128]{2,1,0:T(8,128)(2,1)S(1)} %get-tuple-element.53), channel_id=1, source_target_pairs={{6,0},{59,1},{8,2},{61,3},{10,4},{63,5},{12,6},{1,7},{14,8},{3,9},... | collective-permute-start | bytes 442376 | tf_op jit(solution)/shard_map/ppermute | solution.py:40
  68.2 1.7 %attention.13 = bf16[3,144,128]{2,1,0:T(8,128)(2,1)S(1)} custom-call(s32[258]{0:T(512)S(1)} %pad_add_fusion.1.refs_0_, bf16[3,144,128]{2,1,0:T(8,128)(2,1)S(1)} %collective-permute-done.16.refs_1_, bf16[3,384,512]{2,1,0:T(8,128)(2,1)S(1)} %get-tuple-element.57.refs_2_, bf16[3,192,128]{2,1,0:T(8,128)(2,1)S(1)} %get-tuple-element.39.refs_3_), custom_call_target="tpu_custom_call" | custom-call | flops 84934656 | bytes 1474560 | tf_op jit(solution)/shard_map/attention/pallas_call | solution.py:189
  69.9 3.1 %collective-permute-start.17 = (bf16[3,144,128]{2,1,0:T(8,128)(2,1)S(1)}, bf16[3,144,128]{2,1,0:T(8,128)(2,1)S(1)}, u32[]{:S(2)}, u32[]{:S(2)}) collective-permute-start(bf16[3,144,128]{2,1,0:T(8,128)(2,1)S(1)} %attention.13), channel_id=1, source_target_pairs={{6,0},{59,1},{8,2},{61,3},{10,4},{63,5},{12,6},{1,7},{14,8},{3,9},... | collective-permute-start | bytes 331784 | tf_op jit(solution)/shard_map/ppermute | solution.py:40
  73.0 2.3 %attention.11 = bf16[5,144,128]{2,1,0:T(8,128)(2,1)S(1)} custom-call(s32[258]{0:T(512)S(1)} %pad_add_fusion.1.refs_0_, bf16[5,144,128]{2,1,0:T(8,128)(2,1)S(1)} %collective-permute-done.12.refs_1_, bf16[5,384,512]{2,1,0:T(8,128)(2,1)S(1)} %get-tuple-element.51.refs_2_, bf16[5,192,128]{2,1,0:T(8,128)(2,1)S(1)} %get-tuple-element.52.refs_3_), custom_call_target="tpu_custom_call" | custom-call | flops 141557760 | bytes 2457600 | tf_op jit(solution)/shard_map/attention/pallas_call | solution.py:189
  75.3 8.8 %collective-permute-start.13 = (bf16[5,144,128]{2,1,0:T(8,128)(2,1)S(1)}, bf16[5,144,128]{2,1,0:T(8,128)(2,1)S(1)}, u32[]{:S(2)}, u32[]{:S(2)}) collective-permute-start(bf16[5,144,128]{2,1,0:T(8,128)(2,1)S(1)} %attention.11), channel_id=1, source_target_pairs={{4,0},{61,1},{6,2},{63,3},{8,4},{1,5},{10,6},{3,7},{12,8},{5,9},{1... | collective-permute-start | bytes 552968 | tf_op jit(solution)/shard_map/ppermute | solution.py:40
  84.1 2.3 %attention.10 = bf16[5,144,128]{2,1,0:T(8,128)(2,1)S(1)} custom-call(s32[258]{0:T(512)S(1)} %pad_add_fusion.1.refs_0_, bf16[5,144,128]{2,1,0:T(8,128)(2,1)S(1)} %collective-permute-done.10.refs_1_, bf16[5,384,512]{2,1,0:T(8,128)(2,1)S(1)} %get-tuple-element.49.refs_2_, bf16[5,192,128]{2,1,0:T(8,128)(2,1)S(1)} %get-tuple-element.50.refs_3_), custom_call_target="tpu_custom_call" | custom-call | flops 141557760 | bytes 2457600 | tf_op jit(solution)/shard_map/attention/pallas_call | solution.py:189
  86.5 2.3 %attention.9 = bf16[5,144,128]{2,1,0:T(8,128)(2,1)S(1)} custom-call(s32[258]{0:T(512)S(1)} %pad_add_fusion.1.refs_0_, bf16[5,144,128]{2,1,0:T(8,128)(2,1)S(1)} %collective-permute-done.8.refs_1_, bf16[5,384,512]{2,1,0:T(8,128)(2,1)S(1)} %get-tuple-element.47.refs_2_, bf16[5,192,128]{2,1,0:T(8,128)(2,1)S(1)} %get-tuple-element.48.refs_3_), custom_call_target="tpu_custom_call" | custom-call | flops 141557760 | bytes 2457600 | tf_op jit(solution)/shard_map/attention/pallas_call | solution.py:189
  88.8 6.7 %collective-permute-start.9 = (bf16[5,144,128]{2,1,0:T(8,128)(2,1)S(1)}, bf16[5,144,128]{2,1,0:T(8,128)(2,1)S(1)}, u32[]{:S(2)}, u32[]{:S(2)}) collective-permute-start(bf16[5,144,128]{2,1,0:T(8,128)(2,1)S(1)} %attention.9), channel_id=1, source_target_pairs={{2,0},{63,1},{4,2},{1,3},{6,4},{3,5},{8,6},{5,7},{10,8},{7,9},{12,... | collective-permute-start | bytes 552968 | tf_op jit(solution)/shard_map/ppermute | solution.py:40
  95.5 2.3 %attention.8 = bf16[5,144,128]{2,1,0:T(8,128)(2,1)S(1)} custom-call(s32[258]{0:T(512)S(1)} %pad_add_fusion.1.refs_0_, bf16[5,144,128]{2,1,0:T(8,128)(2,1)S(1)} %collective-permute-done.6.refs_1_, bf16[5,384,512]{2,1,0:T(8,128)(2,1)S(1)} %get-tuple-element.45.refs_2_, bf16[5,192,128]{2,1,0:T(8,128)(2,1)S(1)} %get-tuple-element.46.refs_3_), custom_call_target="tpu_custom_call" | custom-call | flops 141557760 | bytes 2457600 | tf_op jit(solution)/shard_map/attention/pallas_call | solution.py:189
  97.9 1.9 %attention.12 = bf16[4,144,128]{2,1,0:T(8,128)(2,1)S(1)} custom-call(s32[258]{0:T(512)S(1)} %pad_add_fusion.1.refs_0_, bf16[4,144,128]{2,1,0:T(8,128)(2,1)S(1)} %collective-permute-done.14.refs_1_, bf16[4,384,512]{2,1,0:T(8,128)(2,1)S(1)} %get-tuple-element.54.refs_2_, bf16[4,192,128]{2,1,0:T(8,128)(2,1)S(1)} %get-tuple-element.55.refs_3_), custom_call_target="tpu_custom_call" | custom-call | flops 113246208 | bytes 1966080 | tf_op jit(solution)/shard_map/attention/pallas_call | solution.py:189
  100.2 2.3 %attention.7.refs_0_ = bf16[5,144,128]{2,1,0:T(8,128)(2,1)S(1)} custom-call(s32[258]{0:T(512)S(1)} %pad_add_fusion.1.refs_0_, bf16[5,144,128]{2,1,0:T(8,128)(2,1)S(1)} %get-tuple-element.42.refs_1_, bf16[5,384,512]{2,1,0:T(8,128)(2,1)S(1)} %get-tuple-element.43.refs_2_, bf16[5,192,128]{2,1,0:T(8,128)(2,1)S(1)} %get-tuple-element.44.refs_3_), custom_call_target="tpu_custom_call" | custom-call | flops 141557760 | bytes 2457600 | tf_op jit(solution)/shard_map/attention/pallas_call | solution.py:189
  102.5 7.3 %collective-permute-done.15.refs_5_ = bf16[4,144,128]{2,1,0:T(8,128)(2,1)S(1)} collective-permute-done((bf16[4,144,128]{2,1,0:T(8,128)(2,1)S(1)}, bf16[4,144,128]{2,1,0:T(8,128)(2,1)S(1)}, u32[]{:S(2)}, u32[]{:S(2)}) %collective-permute-start.15) | collective-permute-done | bytes 147488 | tf_op jit(solution)/shard_map/ppermute | solution.py:40
  111.8 6.4 %collective-permute-start.20 = (bf16[2,144,128]{2,1,0:T(8,128)(2,1)S(1)}, bf16[2,144,128]{2,1,0:T(8,128)(2,1)S(1)}, u32[]{:S(2)}, u32[]{:S(2)}) collective-permute-start(bf16[2,144,128]{2,1,0:T(8,128)(2,1)S(1)} %get-tuple-element.62), channel_id=1, source_target_pairs={{38,0},{27,1},{40,2},{29,3},{42,4},{31,5},{44,6},{33,7},{46,8},{35... | collective-permute-start | bytes 221192 | tf_op jit(solution)/shard_map/ppermute | solution.py:40
  118.2 4.9 %collective-permute-done.19.refs_0_.refs_1_ = bf16[2,144,128]{2,1,0:T(8,128)(2,1)S(1)} collective-permute-done((bf16[2,144,128]{2,1,0:T(8,128)(2,1)S(1)}, bf16[2,144,128]{2,1,0:T(8,128)(2,1)S(1)}, u32[]{:S(2)}, u32[]{:S(2)}) %collective-permute-start.19) | collective-permute-done | bytes 73760 | tf_op jit(solution)/shard_map/ppermute | solution.py:40
  123.1 11.1 %collective-permute-done.20.refs_1_.refs_2_ = bf16[2,144,128]{2,1,0:T(8,128)(2,1)S(1)} collective-permute-done((bf16[2,144,128]{2,1,0:T(8,128)(2,1)S(1)}, bf16[2,144,128]{2,1,0:T(8,128)(2,1)S(1)}, u32[]{:S(2)}, u32[]{:S(2)}) %collective-permute-start.20) | collective-permute-done | bytes 73760 | tf_op jit(solution)/shard_map/ppermute | solution.py:40
  (57 shorter events, 13.5 us)
Async XLA Ops:
  1.0 0.8 copy-start
  1.7 1.2 collective-permute-start
  3.0 35.0 %collective-permute-start.4 = (bf16[96,64,512]{2,1,0:T(8,128)(2,1)}, bf16[96,64,512]{2,1,0:T(8,128)(2,1)}, u32[]{:S(2)}, u32[]{:S(2)}) collective-permute-start(bf16[96,64,512]{2,1,0:T(8,128)(2,1)} %refs_1_.1), channel_id=1, source_target_pairs={{0,1},{1,0},{2,3},{3,2},{4,5},{5,4},{6,7},{7,6},{8,9},{9,8},{10,11... | collective-permute-start | bytes 18874376 | tf_op jit(solution)/shard_map/ppermute | solution.py:45
  3.1 29.9 %collective-permute-start.1 = (bf16[96,4096]{1,0:T(8,128)(2,1)}, bf16[96,4096]{1,0:T(8,128)(2,1)S(1)}, u32[]{:S(2)}, u32[]{:S(2)}) collective-permute-start(bf16[96,4096]{1,0:T(8,128)(2,1)} %param.9), channel_id=1, source_target_pairs={{0,1},{1,0},{2,3},{3,2},{4,5},{5,4},{6,7},{7,6},{8,9},{9,8},{10,11... | collective-permute-start | bytes 2359304 | tf_op jit(solution)/shard_map/ppermute | solution.py:45
  3.5 40.0 %collective-permute-start.2 = (bf16[2,144,128]{2,1,0:T(8,128)(2,1)S(1)}, bf16[2,144,128]{2,1,0:T(8,128)(2,1)S(1)}, u32[]{:S(2)}, u32[]{:S(2)}) collective-permute-start(bf16[2,144,128]{2,1,0:T(8,128)(2,1)S(1)} %shard_map.64), channel_id=1, source_target_pairs={{12,0},{53,1},{14,2},{55,3},{16,4},{57,5},{18,6},{59,7},{20,8},{61... | collective-permute-start | bytes 221192 | tf_op jit(solution)/shard_map/ppermute | solution.py:40
  28.9 23.0 %collective-permute-start.3 = (bf16[2,144,128]{2,1,0:T(8,128)(2,1)S(1)}, bf16[2,144,128]{2,1,0:T(8,128)(2,1)S(1)}, u32[]{:S(2)}, u32[]{:S(2)}) collective-permute-start(bf16[2,144,128]{2,1,0:T(8,128)(2,1)S(1)} %shard_map.64), channel_id=1, source_target_pairs={{26,0},{39,1},{28,2},{41,3},{30,4},{43,5},{32,6},{45,7},{34,8},{47... | collective-permute-start | bytes 221192 | tf_op jit(solution)/shard_map/ppermute | solution.py:40
  52.0 1.3 collective-permute-start.5
  53.3 16.6 %collective-permute-start.12 = (bf16[5,144,128]{2,1,0:T(8,128)(2,1)S(1)}, bf16[5,144,128]{2,1,0:T(8,128)(2,1)S(1)}, u32[]{:S(2)}, u32[]{:S(2)}) collective-permute-start(bf16[5,144,128]{2,1,0:T(8,128)(2,1)S(1)} %get-tuple-element.42.refs_1_), channel_id=1, source_target_pairs={{60,0},{5,1},{62,2},{7,3},{0,4},{9,5},{2,6},{11,7},{4,8},{13,9},{6... | collective-permute-start | bytes 552968 | tf_op jit(solution)/shard_map/ppermute | solution.py:40
  53.4 11.9 %collective-permute-start.16 = (bf16[3,144,128]{2,1,0:T(8,128)(2,1)S(1)}, bf16[3,144,128]{2,1,0:T(8,128)(2,1)S(1)}, u32[]{:S(2)}, u32[]{:S(2)}) collective-permute-start(bf16[3,144,128]{2,1,0:T(8,128)(2,1)S(1)} %get-tuple-element.56), channel_id=1, source_target_pairs={{58,0},{7,1},{60,2},{9,3},{62,4},{11,5},{0,6},{13,7},{2,8},{15,9},... | collective-permute-start | bytes 331784 | tf_op jit(solution)/shard_map/ppermute | solution.py:40
  55.8 19.5 %collective-permute-start.10 = (bf16[5,144,128]{2,1,0:T(8,128)(2,1)S(1)}, bf16[5,144,128]{2,1,0:T(8,128)(2,1)S(1)}, u32[]{:S(2)}, u32[]{:S(2)}) collective-permute-start(bf16[5,144,128]{2,1,0:T(8,128)(2,1)S(1)} %get-tuple-element.42.refs_1_), channel_id=1, source_target_pairs={{4,0},{61,1},{6,2},{63,3},{8,4},{1,5},{10,6},{3,7},{12,8},{5,9},{1... | collective-permute-start | bytes 552968 | tf_op jit(solution)/shard_map/ppermute | solution.py:40
  57.7 28.6 %collective-permute-start.8 = (bf16[5,144,128]{2,1,0:T(8,128)(2,1)S(1)}, bf16[5,144,128]{2,1,0:T(8,128)(2,1)S(1)}, u32[]{:S(2)}, u32[]{:S(2)}) collective-permute-start(bf16[5,144,128]{2,1,0:T(8,128)(2,1)S(1)} %get-tuple-element.42.refs_1_), channel_id=1, source_target_pairs={{62,0},{3,1},{0,2},{5,3},{2,4},{7,5},{4,6},{9,7},{6,8},{11,9},{8,1... | collective-permute-start | bytes 552968 | tf_op jit(solution)/shard_map/ppermute | solution.py:40
  60.6 28.2 %collective-permute-start.6 = (bf16[5,144,128]{2,1,0:T(8,128)(2,1)S(1)}, bf16[5,144,128]{2,1,0:T(8,128)(2,1)S(1)}, u32[]{:S(2)}, u32[]{:S(2)}) collective-permute-start(bf16[5,144,128]{2,1,0:T(8,128)(2,1)S(1)} %get-tuple-element.42.refs_1_), channel_id=1, source_target_pairs={{2,0},{63,1},{4,2},{1,3},{6,4},{3,5},{8,6},{5,7},{10,8},{7,9},{12,... | collective-permute-start | bytes 552968 | tf_op jit(solution)/shard_map/ppermute | solution.py:40
  65.3 32.4 %collective-permute-start.14 = (bf16[4,144,128]{2,1,0:T(8,128)(2,1)S(1)}, bf16[4,144,128]{2,1,0:T(8,128)(2,1)S(1)}, u32[]{:S(2)}, u32[]{:S(2)}) collective-permute-start(bf16[4,144,128]{2,1,0:T(8,128)(2,1)S(1)} %get-tuple-element.53), channel_id=1, source_target_pairs={{6,0},{59,1},{8,2},{61,3},{10,4},{63,5},{12,6},{1,7},{14,8},{3,9},... | collective-permute-start | bytes 442376 | tf_op jit(solution)/shard_map/ppermute | solution.py:40
  69.9 29.9 %collective-permute-start.17 = (bf16[3,144,128]{2,1,0:T(8,128)(2,1)S(1)}, bf16[3,144,128]{2,1,0:T(8,128)(2,1)S(1)}, u32[]{:S(2)}, u32[]{:S(2)}) collective-permute-start(bf16[3,144,128]{2,1,0:T(8,128)(2,1)S(1)} %attention.13), channel_id=1, source_target_pairs={{6,0},{59,1},{8,2},{61,3},{10,4},{63,5},{12,6},{1,7},{14,8},{3,9},... | collective-permute-start | bytes 331784 | tf_op jit(solution)/shard_map/ppermute | solution.py:40
  75.3 34.5 %collective-permute-start.13 = (bf16[5,144,128]{2,1,0:T(8,128)(2,1)S(1)}, bf16[5,144,128]{2,1,0:T(8,128)(2,1)S(1)}, u32[]{:S(2)}, u32[]{:S(2)}) collective-permute-start(bf16[5,144,128]{2,1,0:T(8,128)(2,1)S(1)} %attention.11), channel_id=1, source_target_pairs={{4,0},{61,1},{6,2},{63,3},{8,4},{1,5},{10,6},{3,7},{12,8},{5,9},{1... | collective-permute-start | bytes 552968 | tf_op jit(solution)/shard_map/ppermute | solution.py:40
  86.4 23.4 %collective-permute-start.11 = (bf16[5,144,128]{2,1,0:T(8,128)(2,1)S(1)}, bf16[5,144,128]{2,1,0:T(8,128)(2,1)S(1)}, u32[]{:S(2)}, u32[]{:S(2)}) collective-permute-start(bf16[5,144,128]{2,1,0:T(8,128)(2,1)S(1)} %attention.10), channel_id=1, source_target_pairs={{60,0},{5,1},{62,2},{7,3},{0,4},{9,5},{2,6},{11,7},{4,8},{13,9},{6... | collective-permute-start | bytes 552968 | tf_op jit(solution)/shard_map/ppermute | solution.py:40
  88.8 21.0 %collective-permute-start.9 = (bf16[5,144,128]{2,1,0:T(8,128)(2,1)S(1)}, bf16[5,144,128]{2,1,0:T(8,128)(2,1)S(1)}, u32[]{:S(2)}, u32[]{:S(2)}) collective-permute-start(bf16[5,144,128]{2,1,0:T(8,128)(2,1)S(1)} %attention.9), channel_id=1, source_target_pairs={{2,0},{63,1},{4,2},{1,3},{6,4},{3,5},{8,6},{5,7},{10,8},{7,9},{12,... | collective-permute-start | bytes 552968 | tf_op jit(solution)/shard_map/ppermute | solution.py:40
  97.8 12.0 %collective-permute-start.7 = (bf16[5,144,128]{2,1,0:T(8,128)(2,1)S(1)}, bf16[5,144,128]{2,1,0:T(8,128)(2,1)S(1)}, u32[]{:S(2)}, u32[]{:S(2)}) collective-permute-start(bf16[5,144,128]{2,1,0:T(8,128)(2,1)S(1)} %attention.8), channel_id=1, source_target_pairs={{62,0},{3,1},{0,2},{5,3},{2,4},{7,5},{4,6},{9,7},{6,8},{11,9},{8,1... | collective-permute-start | bytes 552968 | tf_op jit(solution)/shard_map/ppermute | solution.py:40
  99.9 9.9 %collective-permute-start.15 = (bf16[4,144,128]{2,1,0:T(8,128)(2,1)S(1)}, bf16[4,144,128]{2,1,0:T(8,128)(2,1)S(1)}, u32[]{:S(2)}, u32[]{:S(2)}) collective-permute-start(bf16[4,144,128]{2,1,0:T(8,128)(2,1)S(1)} %attention.12), channel_id=1, source_target_pairs={{58,0},{7,1},{60,2},{9,3},{62,4},{11,5},{0,6},{13,7},{2,8},{15,9},... | collective-permute-start | bytes 442376 | tf_op jit(solution)/shard_map/ppermute | solution.py:40
  110.2 1.4 %collective-permute-start.18 = (bf16[2,144,128]{2,1,0:T(8,128)(2,1)S(1)}, bf16[2,144,128]{2,1,0:T(8,128)(2,1)S(1)}, u32[]{:S(2)}, u32[]{:S(2)}) collective-permute-start(bf16[2,144,128]{2,1,0:T(8,128)(2,1)S(1)} %get-tuple-element.60), channel_id=1, source_target_pairs={{0,1},{1,0},{2,3},{3,2},{4,5},{5,4},{6,7},{7,6},{8,9},{9,8},{10,11... | collective-permute-start | bytes 221192 | tf_op jit(solution)/shard_map/ppermute | solution.py:45
  111.6 11.4 %collective-permute-start.19 = (bf16[2,144,128]{2,1,0:T(8,128)(2,1)S(1)}, bf16[2,144,128]{2,1,0:T(8,128)(2,1)S(1)}, u32[]{:S(2)}, u32[]{:S(2)}) collective-permute-start(bf16[2,144,128]{2,1,0:T(8,128)(2,1)S(1)} %get-tuple-element.61), channel_id=1, source_target_pairs={{52,0},{13,1},{54,2},{15,3},{56,4},{17,5},{58,6},{19,7},{60,8},{21... | collective-permute-start | bytes 221192 | tf_op jit(solution)/shard_map/ppermute | solution.py:40
  111.8 22.4 %collective-permute-start.20 = (bf16[2,144,128]{2,1,0:T(8,128)(2,1)S(1)}, bf16[2,144,128]{2,1,0:T(8,128)(2,1)S(1)}, u32[]{:S(2)}, u32[]{:S(2)}) collective-permute-start(bf16[2,144,128]{2,1,0:T(8,128)(2,1)S(1)} %get-tuple-element.62), channel_id=1, source_target_pairs={{38,0},{27,1},{40,2},{29,3},{42,4},{31,5},{44,6},{33,7},{46,8},{35... | collective-permute-start | bytes 221192 | tf_op jit(solution)/shard_map/ppermute | solution.py:40
  134.2 1.3 collective-permute-start.21
where the time goes:
time: 138 us; the launch traced here: 136 us
  starting transfers between devices  66.5 us (48%)
  waiting for transfers between devices  41.1 us (30%)
  Pallas kernels  21.9 us (16%)
  local copies, waits for them, and re-layouts  5.45 us (4%)
    ppermute x16, starting transfers between devices, shift_from(): return lax.ppermute(array, ('seq', 'head'), pairs)  65.8 us
    ppermute x16, waiting for transfers between devices, shift_from(): return lax.ppermute(array, ('seq', 'head'), pairs)  36.1 us
    pallas_call x7, Pallas kernels, attention(): pl.pallas_call(lambda *refs: attention_kernel(offsets, run_len, count, *r...  15 us
    pallas_call x1, Pallas kernels, gather_pages(): pl.pallas_call(lambda *refs: gather_kernel(run_len, count, *refs), out_sh...  5.55 us
    ppermute x6, waiting for transfers between devices, swapped(): lax.ppermute(array, 'head', [(c, cores - 1 - c) for c in range(cores)])  4.92 us
  transfers between devices with their start and end apart: 22, of which 9 were waited for; matrix products, arithmetic and copies ran while one was open for 4% of the time, Pallas kernels for 15%

commit v1 on v0

--- a/solution.py
+++ b/solution.py
@@ -11,15 +11,16 @@
 ROPE = 64
 NOPE = 128
 LANES = 128
-STAT_ROWS = 16
+ROPE_ROWS = 16
+STAT_ROWS = 8
 MASKED_SCORE = -1e30
 
 FAR = (0, 6, 13, -6, -13)
 NEAR = {
+    2: FAR,
+    -2: FAR,
     1: FAR,
     -1: FAR,
-    2: FAR,
-    -2: FAR,
     3: (0, 6, 13, -13),
     -3: (0, 13, -6),
 }
@@ -125,13 +126,13 @@
 
 def attention_kernel(offsets, run_len, count, table_ref, q_ref, keys_ref, rotary_ref, out_ref):
     tokens, width = keys_ref.shape[1:]
-    packed = q_ref.shape[1] - STAT_ROWS
+    packed = q_ref.shape[1] - ROPE_ROWS
     slabs = width // LANES
     heads = packed // slabs
     half = tokens // 2
     entry = 2 * (run_len + 1)
     lane = lax.broadcasted_iota(jnp.int32, (heads, LANES), 1)
-    rope_lane = lax.broadcasted_iota(jnp.int32, (STAT_ROWS, LANES), 1)
+    rope_lane = lax.broadcasted_iota(jnp.int32, (ROPE_ROWS, LANES), 1)
     column = lax.broadcasted_iota(jnp.int32, (heads, tokens), 1)
     row_of = lax.broadcasted_iota(jnp.int32, (tokens, tokens // 2), 0) // 2
     row_in = lax.broadcasted_iota(jnp.int32, (tokens, tokens // 2), 1)
@@ -184,11 +185,12 @@
 def attention(offsets, table, queries, pages, run_len, count):
     groups, rows, _ = queries.shape
     tokens, width = pages[0].shape[1:]
-    heads = (rows - STAT_ROWS) * LANES // width
+    packed = rows - ROPE_ROWS
+    heads = packed * LANES // width
     work = groups * tokens
     return pl.pallas_call(
         lambda *refs: attention_kernel(offsets, run_len, count, *refs),
-        out_shape=jax.ShapeDtypeStruct((groups, rows, LANES), jnp.bfloat16),
+        out_shape=jax.ShapeDtypeStruct((groups, packed + STAT_ROWS, LANES), jnp.bfloat16),
         in_specs=[pl.BlockSpec(memory_space=pltpu.SMEM)] + [VMEM] * 3,
         out_specs=VMEM,
         compiler_params=LIMIT,
@@ -265,7 +267,8 @@
 
     rope_rows = q_rope.reshape(2, heads // 2, rope_width)
     rope_rows = jnp.concatenate([rope_rows[0], rope_rows[1]], axis=1)
-    block_shape = (1, heads * latent_width // LANES + STAT_ROWS, LANES)
+    packed = heads * latent_width // LANES
+    block_shape = (1, packed + ROPE_ROWS, LANES)
     block = pl.pallas_call(
         pack_kernel,
         out_shape=jax.ShapeDtypeStruct(block_shape, jnp.bfloat16),
@@ -313,22 +316,24 @@
     six, thirteen, _ = lax.optimization_barrier((six, thirteen, pages[-1][1]))
     crossing = swapped(joined([six, thirteen], ((0, 1), (1, 1))))
     where = {0: (0, 0), 6: (1, 0), 13: (2, 0), -6: (3, 0), -13: (3, 1)}
-    lists = [held for held in dict.fromkeys(held for _, held in GROUPS)]
-    fars = joined([block, six, thirteen, crossing], *[[where[o] for o in held] for held in lists])
-    fars = dict(zip(lists, fars))
-
-    near = {d: shift_from(fars[held], d) for d, held in NEAR.items()}
+    far = joined([block, six, thirteen, crossing], [where[o] for o in FAR])
+
+    near = {d: shift_from(far, d) for d in (2, -2, 1, -1)}
+    for d in (3, -3):
+        step = d // 3
+        onward = joined([near[2 * step]], [(0, FAR.index(o)) for o in NEAR[d]])
+        near[d] = shift_from(onward, step)
     partials, sources = [], []
     for (d, held), group_pages in zip(GROUPS, pages):
         offsets = tuple(o + d for o in held)
-        queries = near[d] if d else fars[held]
+        queries = near[d] if d else far
         partial = attention(offsets, table, queries, group_pages, run_len, seq_count)
         partials.append(shift_from(partial, -d) if d else partial)
         sources.append(held)
 
     home, ahead, across = pl.pallas_call(
         lambda *refs: near_merge_kernel(heads, sources, *refs),
-        out_shape=[jax.ShapeDtypeStruct((n,) + block_shape[1:], jnp.bfloat16) for n in (1, 2, 2)],
+        out_shape=[jax.ShapeDtypeStruct((n, packed + STAT_ROWS, LANES), jnp.bfloat16) for n in (1, 2, 2)],
         in_specs=[VMEM] * len(sources),
         out_specs=[VMEM] * 3,
         compiler_params=LIMIT,

time: 138 us -> 136 us (0.986)
  waiting for transfers between devices: 41.1 us -> 26.3 us
  starting transfers between devices: 66.5 us -> 80.1 us
    ppermute x16, waiting for transfers between devices: 36.1 us -> 22.1 us  [shift_from(): return lax.ppermute(array, ('seq', 'head'), pairs)]
    ppermute x6, starting transfers between devices: 0.69 us -> 12.5 us  [swapped(): lax.ppermute(array, 'head', [(c, cores - 1 - c) for c in range(cores)])]
    ppermute x16, starting transfers between devices: 65.8 us -> 67.5 us  [shift_from(): return lax.ppermute(array, ('seq', 'head'), pairs)]
where the time goes in v1:
time: 136 us; the launch traced here: 135 us
  starting transfers between devices  80.1 us (59%)
  waiting for transfers between devices  26.3 us (19%)
  Pallas kernels  21.8 us (16%)
  local copies, waits for them, and re-layouts  5.45 us (4%)
    ppermute x16, starting transfers between devices, shift_from(): return lax.ppermute(array, ('seq', 'head'), pairs)  67.5 us
    ppermute x16, waiting for transfers between devices, shift_from(): return lax.ppermute(array, ('seq', 'head'), pairs)  22.1 us
    pallas_call x7, Pallas kernels, attention(): pl.pallas_call(lambda *refs: attention_kernel(offsets, run_len, count, *r...  15 us
    ppermute x6, starting transfers between devices, swapped(): lax.ppermute(array, 'head', [(c, cores - 1 - c) for c in range(cores)])  12.5 us
    pallas_call x1, Pallas kernels, gather_pages(): pl.pallas_call(lambda *refs: gather_kernel(run_len, count, *refs), out_sh...  5.55 us
    ppermute x6, waiting for transfers between devices, swapped(): lax.ppermute(array, 'head', [(c, cores - 1 - c) for c in range(cores)])  4.26 us
  transfers between devices with their start and end apart: 22, of which 9 were waited for; matrix products, arithmetic and copies ran while one was open for 4% of the time, Pallas kernels for 15%

profile of v1, /device:TPU:38, one launch (start us, length us, event | category | flops | bytes accessed | tf_op | source)
XLA Modules:
  0.0 135.0 jit_solution(12700435140516677790)
XLA Ops:
  3.5 25.5 %collective-permute-start.2 = (bf16[2,144,128]{2,1,0:T(8,128)(2,1)S(1)}, bf16[2,144,128]{2,1,0:T(8,128)(2,1)S(1)}, u32[]{:S(2)}, u32[]{:S(2)}) collective-permute-start(bf16[2,144,128]{2,1,0:T(8,128)(2,1)S(1)} %shard_map.64), channel_id=1, source_target_pairs={{12,0},{53,1},{14,2},{55,3},{16,4},{57,5},{18,6},{59,7},{20,8},{61... | collective-permute-start | bytes 221192 | tf_op jit(solution)/shard_map/ppermute | solution.py:41
  28.9 4.1 %collective-permute-start.3 = (bf16[2,144,128]{2,1,0:T(8,128)(2,1)S(1)}, bf16[2,144,128]{2,1,0:T(8,128)(2,1)S(1)}, u32[]{:S(2)}, u32[]{:S(2)}) collective-permute-start(bf16[2,144,128]{2,1,0:T(8,128)(2,1)S(1)} %shard_map.64), channel_id=1, source_target_pairs={{26,0},{39,1},{28,2},{41,3},{30,4},{43,5},{32,6},{45,7},{34,8},{47... | collective-permute-start | bytes 221192 | tf_op jit(solution)/shard_map/ppermute | solution.py:41
  37.9 5.6 %gather_pages.1 = (bf16[5,384,512]{2,1,0:T(8,128)(2,1)S(1)}, bf16[5,192,128]{2,1,0:T(8,128)(2,1)S(1)}, bf16[5,384,512]{2,1,0:T(8,128)(2,1)S(1)}, bf16[5,192,128]...) custom-call(s32[258]{0:T(512)S(1)} %pad_add_fusion.1.refs_0_, ...), custom_call_target="tpu_custom_call" | custom-call | flops 4294967296 | bytes 28311552 | tf_op jit(solution)/shard_map/gather_pages/pallas_call | solution.py:112
  43.5 8.5 %collective-permute-done.3.refs_1_.refs_2_ = bf16[2,144,128]{2,1,0:T(8,128)(2,1)S(1)} collective-permute-done((bf16[2,144,128]{2,1,0:T(8,128)(2,1)S(1)}, bf16[2,144,128]{2,1,0:T(8,128)(2,1)S(1)}, u32[]{:S(2)}, u32[]{:S(2)}) %collective-permute-start.3) | collective-permute-done | bytes 73760 | tf_op jit(solution)/shard_map/ppermute | solution.py:41
  53.4 4.1 %collective-permute-start.12 = (bf16[5,144,128]{2,1,0:T(8,128)(2,1)S(1)}, bf16[5,144,128]{2,1,0:T(8,128)(2,1)S(1)}, u32[]{:S(2)}, u32[]{:S(2)}) collective-permute-start(bf16[5,144,128]{2,1,0:T(8,128)(2,1)S(1)} %shard_map.66.refs_1_), channel_id=1, source_target_pairs={{62,0},{3,1},{0,2},{5,3},{2,4},{7,5},{4,6},{9,7},{6,8},{11,9},{8,1... | collective-permute-start | bytes 552968 | tf_op jit(solution)/shard_map/ppermute | solution.py:41
  57.5 2.7 %collective-permute-start.10 = (bf16[5,144,128]{2,1,0:T(8,128)(2,1)S(1)}, bf16[5,144,128]{2,1,0:T(8,128)(2,1)S(1)}, u32[]{:S(2)}, u32[]{:S(2)}) collective-permute-start(bf16[5,144,128]{2,1,0:T(8,128)(2,1)S(1)} %shard_map.66.refs_1_), channel_id=1, source_target_pairs={{2,0},{63,1},{4,2},{1,3},{6,4},{3,5},{8,6},{5,7},{10,8},{7,9},{12,... | collective-permute-start | bytes 552968 | tf_op jit(solution)/shard_map/ppermute | solution.py:41
  60.2 3.6 %collective-permute-done.6.refs_1_.refs_0_ = bf16[5,144,128]{2,1,0:T(8,128)(2,1)S(1)} collective-permute-done((bf16[5,144,128]{2,1,0:T(8,128)(2,1)S(1)}, bf16[5,144,128]{2,1,0:T(8,128)(2,1)S(1)}, u32[]{:S(2)}, u32[]{:S(2)}) %collective-permute-start.6) | collective-permute-done | bytes 184352 | tf_op jit(solution)/shard_map/ppermute | solution.py:41
  63.9 4.6 %collective-permute-start.14 = (bf16[4,144,128]{2,1,0:T(8,128)(2,1)S(1)}, bf16[4,144,128]{2,1,0:T(8,128)(2,1)S(1)}, u32[]{:S(2)}, u32[]{:S(2)}) collective-permute-start(bf16[4,144,128]{2,1,0:T(8,128)(2,1)S(1)} %shard_map.67), channel_id=1, source_target_pairs={{2,0},{63,1},{4,2},{1,3},{6,4},{3,5},{8,6},{5,7},{10,8},{7,9},{12,... | collective-permute-start | bytes 442376 | tf_op jit(solution)/shard_map/ppermute | solution.py:41
  68.5 2.3 %attention.11 = bf16[5,136,128]{2,1,0:T(8,128)(2,1)S(1)} custom-call(s32[258]{0:T(512)S(1)} %pad_add_fusion.1.refs_0_, bf16[5,144,128]{2,1,0:T(8,128)(2,1)S(1)} %collective-permute-done.12.refs_1_, bf16[5,384,512]{2,1,0:T(8,128)(2,1)S(1)} %get-tuple-element.47.refs_2_, bf16[5,192,128]{2,1,0:T(8,128)(2,1)S(1)} %get-tuple-element.48.refs_3_), custom_call_target="tpu_custom_call" | custom-call | flops 141557760 | bytes 2457600 | tf_op jit(solution)/shard_map/attention/pallas_call | solution.py:191
  71.3 1.8 %collective-permute-start.16 = (bf16[3,144,128]{2,1,0:T(8,128)(2,1)S(1)}, bf16[3,144,128]{2,1,0:T(8,128)(2,1)S(1)}, u32[]{:S(2)}, u32[]{:S(2)}) collective-permute-start(bf16[3,144,128]{2,1,0:T(8,128)(2,1)S(1)} %shard_map.68), channel_id=1, source_target_pairs={{62,0},{3,1},{0,2},{5,3},{2,4},{7,5},{4,6},{9,7},{6,8},{11,9},{8,1... | collective-permute-start | bytes 331784 | tf_op jit(solution)/shard_map/ppermute | solution.py:41
  73.1 2.3 %attention.10 = bf16[5,136,128]{2,1,0:T(8,128)(2,1)S(1)} custom-call(s32[258]{0:T(512)S(1)} %pad_add_fusion.1.refs_0_, bf16[5,144,128]{2,1,0:T(8,128)(2,1)S(1)} %collective-permute-done.10.refs_1_, bf16[5,384,512]{2,1,0:T(8,128)(2,1)S(1)} %get-tuple-element.45.refs_2_, bf16[5,192,128]{2,1,0:T(8,128)(2,1)S(1)} %get-tuple-element.46.refs_3_), custom_call_target="tpu_custom_call" | custom-call | flops 141557760 | bytes 2457600 | tf_op jit(solution)/shard_map/attention/pallas_call | solution.py:191
  75.6 2.3 %attention.9 = bf16[5,136,128]{2,1,0:T(8,128)(2,1)S(1)} custom-call(s32[258]{0:T(512)S(1)} %pad_add_fusion.1.refs_0_, bf16[5,144,128]{2,1,0:T(8,128)(2,1)S(1)} %collective-permute-done.8.refs_1_.refs_0_, bf16[5,384,512]{2,1,0:T(8,128)(2,1)S(1)} %get-tuple-element.43.refs_2_, bf16[5,192,128]{2,1,0:T(8,128)(2,1)S(1)} %get-tuple-element.44.refs_3_), custom_call_target="tpu_custom_call" | custom-call | flops 141557760 | bytes 2457600 | tf_op jit(solution)/shard_map/attention/pallas_call | solution.py:191
  77.9 2.9 %collective-permute-start.9 = (bf16[5,136,128]{2,1,0:T(8,128)(2,1)S(1)}, bf16[5,136,128]{2,1,0:T(8,128)(2,1)S(1)}, u32[]{:S(2)}, u32[]{:S(2)}) collective-permute-start(bf16[5,136,128]{2,1,0:T(8,128)(2,1)S(1)} %attention.9), channel_id=1, source_target_pairs={{4,0},{61,1},{6,2},{63,3},{8,4},{1,5},{10,6},{3,7},{12,8},{5,9},{1... | collective-permute-start | bytes 522248 | tf_op jit(solution)/shard_map/ppermute | solution.py:41
  80.8 2.3 %attention.8 = bf16[5,136,128]{2,1,0:T(8,128)(2,1)S(1)} custom-call(s32[258]{0:T(512)S(1)} %pad_add_fusion.1.refs_0_, bf16[5,144,128]{2,1,0:T(8,128)(2,1)S(1)} %collective-permute-done.6.refs_1_.refs_0_, bf16[5,384,512]{2,1,0:T(8,128)(2,1)S(1)} %get-tuple-element.41.refs_2_, bf16[5,192,128]{2,1,0:T(8,128)(2,1)S(1)} %get-tuple-element.42.refs_3_), custom_call_target="tpu_custom_call" | custom-call | flops 141557760 | bytes 2457600 | tf_op jit(solution)/shard_map/attention/pallas_call | solution.py:191
  83.3 1.9 %attention.12 = bf16[4,136,128]{2,1,0:T(8,128)(2,1)S(1)} custom-call(s32[258]{0:T(512)S(1)} %pad_add_fusion.1.refs_0_, bf16[4,144,128]{2,1,0:T(8,128)(2,1)S(1)} %collective-permute-done.14.refs_1_, bf16[4,384,512]{2,1,0:T(8,128)(2,1)S(1)} %get-tuple-element.49.refs_2_, bf16[4,192,128]{2,1,0:T(8,128)(2,1)S(1)} %get-tuple-element.50.refs_3_), custom_call_target="tpu_custom_call" | custom-call | flops 113246208 | bytes 1966080 | tf_op jit(solution)/shard_map/attention/pallas_call | solution.py:191
  85.3 1.6 %collective-permute-start.15 = (bf16[4,136,128]{2,1,0:T(8,128)(2,1)S(1)}, bf16[4,136,128]{2,1,0:T(8,128)(2,1)S(1)}, u32[]{:S(2)}, u32[]{:S(2)}) collective-permute-start(bf16[4,136,128]{2,1,0:T(8,128)(2,1)S(1)} %attention.12), channel_id=1, source_target_pairs={{58,0},{7,1},{60,2},{9,3},{62,4},{11,5},{0,6},{13,7},{2,8},{15,9},... | collective-permute-start | bytes 417800 | tf_op jit(solution)/shard_map/ppermute | solution.py:41
  86.8 1.7 %attention.13 = bf16[3,136,128]{2,1,0:T(8,128)(2,1)S(1)} custom-call(s32[258]{0:T(512)S(1)} %pad_add_fusion.1.refs_0_, bf16[3,144,128]{2,1,0:T(8,128)(2,1)S(1)} %collective-permute-done.16.refs_1_, bf16[3,384,512]{2,1,0:T(8,128)(2,1)S(1)} %get-tuple-element.51.refs_2_, bf16[3,192,128]{2,1,0:T(8,128)(2,1)S(1)} %get-tuple-element.36.refs_3_), custom_call_target="tpu_custom_call" | custom-call | flops 84934656 | bytes 1474560 | tf_op jit(solution)/shard_map/attention/pallas_call | solution.py:191
  88.5 3.9 %collective-permute-start.17 = (bf16[3,136,128]{2,1,0:T(8,128)(2,1)S(1)}, bf16[3,136,128]{2,1,0:T(8,128)(2,1)S(1)}, u32[]{:S(2)}, u32[]{:S(2)}) collective-permute-start(bf16[3,136,128]{2,1,0:T(8,128)(2,1)S(1)} %attention.13), channel_id=1, source_target_pairs={{6,0},{59,1},{8,2},{61,3},{10,4},{63,5},{12,6},{1,7},{14,8},{3,9},... | collective-permute-start | bytes 313352 | tf_op jit(solution)/shard_map/ppermute | solution.py:41
  92.5 2.3 %attention.7.refs_0_ = bf16[5,136,128]{2,1,0:T(8,128)(2,1)S(1)} custom-call(s32[258]{0:T(512)S(1)} %pad_add_fusion.1.refs_0_, bf16[5,144,128]{2,1,0:T(8,128)(2,1)S(1)} %shard_map.66.refs_1_, bf16[5,384,512]{2,1,0:T(8,128)(2,1)S(1)} %get-tuple-element.39.refs_2_, bf16[5,192,128]{2,1,0:T(8,128)(2,1)S(1)} %get-tuple-element.40.refs_3_), custom_call_target="tpu_custom_call" | custom-call | flops 141557760 | bytes 2457600 | tf_op jit(solution)/shard_map/attention/pallas_call | solution.py:191
  94.8 3.0 %collective-permute-done.17.refs_6_ = bf16[3,136,128]{2,1,0:T(8,128)(2,1)S(1)} collective-permute-done((bf16[3,136,128]{2,1,0:T(8,128)(2,1)S(1)}, bf16[3,136,128]{2,1,0:T(8,128)(2,1)S(1)}, u32[]{:S(2)}, u32[]{:S(2)}) %collective-permute-start.17) | collective-permute-done | bytes 104480 | tf_op jit(solution)/shard_map/ppermute | solution.py:41
  98.2 2.4 %collective-permute-start.18 = (bf16[2,136,128]{2,1,0:T(8,128)(2,1)S(1)}, bf16[2,136,128]{2,1,0:T(8,128)(2,1)S(1)}, u32[]{:S(2)}, u32[]{:S(2)}) collective-permute-start(bf16[2,136,128]{2,1,0:T(8,128)(2,1)S(1)} %get-tuple-element.54), channel_id=1, source_target_pairs={{0,1},{1,0},{2,3},{3,2},{4,5},{5,4},{6,7},{7,6},{8,9},{9,8},{10,11... | collective-permute-start | bytes 208904 | tf_op jit(solution)/shard_map/ppermute | solution.py:46
  102.0 15.1 %collective-permute-start.20 = (bf16[2,136,128]{2,1,0:T(8,128)(2,1)S(1)}, bf16[2,136,128]{2,1,0:T(8,128)(2,1)S(1)}, u32[]{:S(2)}, u32[]{:S(2)}) collective-permute-start(bf16[2,136,128]{2,1,0:T(8,128)(2,1)S(1)} %get-tuple-element.56), channel_id=1, source_target_pairs={{38,0},{27,1},{40,2},{29,3},{42,4},{31,5},{44,6},{33,7},{46,8},{35... | collective-permute-start | bytes 208904 | tf_op jit(solution)/shard_map/ppermute | solution.py:41
  117.1 6.6 %collective-permute-done.20.refs_1_.refs_2_ = bf16[2,136,128]{2,1,0:T(8,128)(2,1)S(1)} collective-permute-done((bf16[2,136,128]{2,1,0:T(8,128)(2,1)S(1)}, bf16[2,136,128]{2,1,0:T(8,128)(2,1)S(1)}, u32[]{:S(2)}, u32[]{:S(2)}) %collective-permute-start.20) | collective-permute-done | bytes 69664 | tf_op jit(solution)/shard_map/ppermute | solution.py:41
  123.7 9.6 %collective-permute-start.21 = (bf16[2,136,128]{2,1,0:T(8,128)(2,1)S(1)}, bf16[2,136,128]{2,1,0:T(8,128)(2,1)S(1)}, u32[]{:S(2)}, u32[]{:S(2)}) collective-permute-start(bf16[2,136,128]{2,1,0:T(8,128)(2,1)S(1)} %shard_map.70), channel_id=1, source_target_pairs={{0,1},{1,0},{2,3},{3,2},{4,5},{5,4},{6,7},{7,6},{8,9},{9,8},{10,11... | collective-permute-start | bytes 208904 | tf_op jit(solution)/shard_map/ppermute | solution.py:46
  (59 shorter events, 14.2 us)
Async XLA Ops:
  1.0 0.8 copy-start
  1.7 1.2 collective-permute-start
  3.0 35.0 %collective-permute-start.4 = (bf16[96,64,512]{2,1,0:T(8,128)(2,1)}, bf16[96,64,512]{2,1,0:T(8,128)(2,1)}, u32[]{:S(2)}, u32[]{:S(2)}) collective-permute-start(bf16[96,64,512]{2,1,0:T(8,128)(2,1)} %refs_1_.1), channel_id=1, source_target_pairs={{0,1},{1,0},{2,3},{3,2},{4,5},{5,4},{6,7},{7,6},{8,9},{9,8},{10,11... | collective-permute-start | bytes 18874376 | tf_op jit(solution)/shard_map/ppermute | solution.py:46
  3.1 29.9 %collective-permute-start.1 = (bf16[96,4096]{1,0:T(8,128)(2,1)}, bf16[96,4096]{1,0:T(8,128)(2,1)S(1)}, u32[]{:S(2)}, u32[]{:S(2)}) collective-permute-start(bf16[96,4096]{1,0:T(8,128)(2,1)} %param.9), channel_id=1, source_target_pairs={{0,1},{1,0},{2,3},{3,2},{4,5},{5,4},{6,7},{7,6},{8,9},{9,8},{10,11... | collective-permute-start | bytes 2359304 | tf_op jit(solution)/shard_map/ppermute | solution.py:46
  3.5 40.0 %collective-permute-start.2 = (bf16[2,144,128]{2,1,0:T(8,128)(2,1)S(1)}, bf16[2,144,128]{2,1,0:T(8,128)(2,1)S(1)}, u32[]{:S(2)}, u32[]{:S(2)}) collective-permute-start(bf16[2,144,128]{2,1,0:T(8,128)(2,1)S(1)} %shard_map.64), channel_id=1, source_target_pairs={{12,0},{53,1},{14,2},{55,3},{16,4},{57,5},{18,6},{59,7},{20,8},{61... | collective-permute-start | bytes 221192 | tf_op jit(solution)/shard_map/ppermute | solution.py:41
  28.9 23.0 %collective-permute-start.3 = (bf16[2,144,128]{2,1,0:T(8,128)(2,1)S(1)}, bf16[2,144,128]{2,1,0:T(8,128)(2,1)S(1)}, u32[]{:S(2)}, u32[]{:S(2)}) collective-permute-start(bf16[2,144,128]{2,1,0:T(8,128)(2,1)S(1)} %shard_map.64), channel_id=1, source_target_pairs={{26,0},{39,1},{28,2},{41,3},{30,4},{43,5},{32,6},{45,7},{34,8},{47... | collective-permute-start | bytes 221192 | tf_op jit(solution)/shard_map/ppermute | solution.py:41
  52.0 1.3 collective-permute-start.5
  53.3 10.6 %collective-permute-start.6 = (bf16[5,144,128]{2,1,0:T(8,128)(2,1)S(1)}, bf16[5,144,128]{2,1,0:T(8,128)(2,1)S(1)}, u32[]{:S(2)}, u32[]{:S(2)}) collective-permute-start(bf16[5,144,128]{2,1,0:T(8,128)(2,1)S(1)} %shard_map.66.refs_1_), channel_id=1, source_target_pairs={{4,0},{61,1},{6,2},{63,3},{8,4},{1,5},{10,6},{3,7},{12,8},{5,9},{1... | collective-permute-start | bytes 552968 | tf_op jit(solution)/shard_map/ppermute | solution.py:41
  53.4 15.1 %collective-permute-start.12 = (bf16[5,144,128]{2,1,0:T(8,128)(2,1)S(1)}, bf16[5,144,128]{2,1,0:T(8,128)(2,1)S(1)}, u32[]{:S(2)}, u32[]{:S(2)}) collective-permute-start(bf16[5,144,128]{2,1,0:T(8,128)(2,1)S(1)} %shard_map.66.refs_1_), channel_id=1, source_target_pairs={{62,0},{3,1},{0,2},{5,3},{2,4},{7,5},{4,6},{9,7},{6,8},{11,9},{8,1... | collective-permute-start | bytes 552968 | tf_op jit(solution)/shard_map/ppermute | solution.py:41
  57.5 13.7 %collective-permute-start.8 = (bf16[5,144,128]{2,1,0:T(8,128)(2,1)S(1)}, bf16[5,144,128]{2,1,0:T(8,128)(2,1)S(1)}, u32[]{:S(2)}, u32[]{:S(2)}) collective-permute-start(bf16[5,144,128]{2,1,0:T(8,128)(2,1)S(1)} %shard_map.66.refs_1_), channel_id=1, source_target_pairs={{60,0},{5,1},{62,2},{7,3},{0,4},{9,5},{2,6},{11,7},{4,8},{13,9},{6... | collective-permute-start | bytes 552968 | tf_op jit(solution)/shard_map/ppermute | solution.py:41
  57.5 15.5 %collective-permute-start.10 = (bf16[5,144,128]{2,1,0:T(8,128)(2,1)S(1)}, bf16[5,144,128]{2,1,0:T(8,128)(2,1)S(1)}, u32[]{:S(2)}, u32[]{:S(2)}) collective-permute-start(bf16[5,144,128]{2,1,0:T(8,128)(2,1)S(1)} %shard_map.66.refs_1_), channel_id=1, source_target_pairs={{2,0},{63,1},{4,2},{1,3},{6,4},{3,5},{8,6},{5,7},{10,8},{7,9},{12,... | collective-permute-start | bytes 552968 | tf_op jit(solution)/shard_map/ppermute | solution.py:41
  63.9 19.3 %collective-permute-start.14 = (bf16[4,144,128]{2,1,0:T(8,128)(2,1)S(1)}, bf16[4,144,128]{2,1,0:T(8,128)(2,1)S(1)}, u32[]{:S(2)}, u32[]{:S(2)}) collective-permute-start(bf16[4,144,128]{2,1,0:T(8,128)(2,1)S(1)} %shard_map.67), channel_id=1, source_target_pairs={{2,0},{63,1},{4,2},{1,3},{6,4},{3,5},{8,6},{5,7},{10,8},{7,9},{12,... | collective-permute-start | bytes 442376 | tf_op jit(solution)/shard_map/ppermute | solution.py:41
  70.8 17.7 %collective-permute-start.13 = (bf16[5,136,128]{2,1,0:T(8,128)(2,1)S(1)}, bf16[5,136,128]{2,1,0:T(8,128)(2,1)S(1)}, u32[]{:S(2)}, u32[]{:S(2)}) collective-permute-start(bf16[5,136,128]{2,1,0:T(8,128)(2,1)S(1)} %attention.11), channel_id=1, source_target_pairs={{2,0},{63,1},{4,2},{1,3},{6,4},{3,5},{8,6},{5,7},{10,8},{7,9},{12,... | collective-permute-start | bytes 522248 | tf_op jit(solution)/shard_map/ppermute | solution.py:41
  71.3 14.0 %collective-permute-start.16 = (bf16[3,144,128]{2,1,0:T(8,128)(2,1)S(1)}, bf16[3,144,128]{2,1,0:T(8,128)(2,1)S(1)}, u32[]{:S(2)}, u32[]{:S(2)}) collective-permute-start(bf16[3,144,128]{2,1,0:T(8,128)(2,1)S(1)} %shard_map.68), channel_id=1, source_target_pairs={{62,0},{3,1},{0,2},{5,3},{2,4},{7,5},{4,6},{9,7},{6,8},{11,9},{8,1... | collective-permute-start | bytes 331784 | tf_op jit(solution)/shard_map/ppermute | solution.py:41
  75.3 19.4 %collective-permute-start.11 = (bf16[5,136,128]{2,1,0:T(8,128)(2,1)S(1)}, bf16[5,136,128]{2,1,0:T(8,128)(2,1)S(1)}, u32[]{:S(2)}, u32[]{:S(2)}) collective-permute-start(bf16[5,136,128]{2,1,0:T(8,128)(2,1)S(1)} %attention.10), channel_id=1, source_target_pairs={{62,0},{3,1},{0,2},{5,3},{2,4},{7,5},{4,6},{9,7},{6,8},{11,9},{8,1... | collective-permute-start | bytes 522248 | tf_op jit(solution)/shard_map/ppermute | solution.py:41
  77.9 16.9 %collective-permute-start.9 = (bf16[5,136,128]{2,1,0:T(8,128)(2,1)S(1)}, bf16[5,136,128]{2,1,0:T(8,128)(2,1)S(1)}, u32[]{:S(2)}, u32[]{:S(2)}) collective-permute-start(bf16[5,136,128]{2,1,0:T(8,128)(2,1)S(1)} %attention.9), channel_id=1, source_target_pairs={{4,0},{61,1},{6,2},{63,3},{8,4},{1,5},{10,6},{3,7},{12,8},{5,9},{1... | collective-permute-start | bytes 522248 | tf_op jit(solution)/shard_map/ppermute | solution.py:41
  83.1 11.6 %collective-permute-start.7 = (bf16[5,136,128]{2,1,0:T(8,128)(2,1)S(1)}, bf16[5,136,128]{2,1,0:T(8,128)(2,1)S(1)}, u32[]{:S(2)}, u32[]{:S(2)}) collective-permute-start(bf16[5,136,128]{2,1,0:T(8,128)(2,1)S(1)} %attention.8), channel_id=1, source_target_pairs={{60,0},{5,1},{62,2},{7,3},{0,4},{9,5},{2,6},{11,7},{4,8},{13,9},{6... | collective-permute-start | bytes 522248 | tf_op jit(solution)/shard_map/ppermute | solution.py:41
  85.3 12.5 %collective-permute-start.15 = (bf16[4,136,128]{2,1,0:T(8,128)(2,1)S(1)}, bf16[4,136,128]{2,1,0:T(8,128)(2,1)S(1)}, u32[]{:S(2)}, u32[]{:S(2)}) collective-permute-start(bf16[4,136,128]{2,1,0:T(8,128)(2,1)S(1)} %attention.12), channel_id=1, source_target_pairs={{58,0},{7,1},{60,2},{9,3},{62,4},{11,5},{0,6},{13,7},{2,8},{15,9},... | collective-permute-start | bytes 417800 | tf_op jit(solution)/shard_map/ppermute | solution.py:41
  88.5 9.3 %collective-permute-start.17 = (bf16[3,136,128]{2,1,0:T(8,128)(2,1)S(1)}, bf16[3,136,128]{2,1,0:T(8,128)(2,1)S(1)}, u32[]{:S(2)}, u32[]{:S(2)}) collective-permute-start(bf16[3,136,128]{2,1,0:T(8,128)(2,1)S(1)} %attention.13), channel_id=1, source_target_pairs={{6,0},{59,1},{8,2},{61,3},{10,4},{63,5},{12,6},{1,7},{14,8},{3,9},... | collective-permute-start | bytes 313352 | tf_op jit(solution)/shard_map/ppermute | solution.py:41
  98.2 3.3 %collective-permute-start.18 = (bf16[2,136,128]{2,1,0:T(8,128)(2,1)S(1)}, bf16[2,136,128]{2,1,0:T(8,128)(2,1)S(1)}, u32[]{:S(2)}, u32[]{:S(2)}) collective-permute-start(bf16[2,136,128]{2,1,0:T(8,128)(2,1)S(1)} %get-tuple-element.54), channel_id=1, source_target_pairs={{0,1},{1,0},{2,3},{3,2},{4,5},{5,4},{6,7},{7,6},{8,9},{9,8},{10,11... | collective-permute-start | bytes 208904 | tf_op jit(solution)/shard_map/ppermute | solution.py:46
  101.6 15.5 %collective-permute-start.19 = (bf16[2,136,128]{2,1,0:T(8,128)(2,1)S(1)}, bf16[2,136,128]{2,1,0:T(8,128)(2,1)S(1)}, u32[]{:S(2)}, u32[]{:S(2)}) collective-permute-start(bf16[2,136,128]{2,1,0:T(8,128)(2,1)S(1)} %get-tuple-element.55), channel_id=1, source_target_pairs={{52,0},{13,1},{54,2},{15,3},{56,4},{17,5},{58,6},{19,7},{60,8},{21... | collective-permute-start | bytes 208904 | tf_op jit(solution)/shard_map/ppermute | solution.py:41
  102.0 21.7 %collective-permute-start.20 = (bf16[2,136,128]{2,1,0:T(8,128)(2,1)S(1)}, bf16[2,136,128]{2,1,0:T(8,128)(2,1)S(1)}, u32[]{:S(2)}, u32[]{:S(2)}) collective-permute-start(bf16[2,136,128]{2,1,0:T(8,128)(2,1)S(1)} %get-tuple-element.56), channel_id=1, source_target_pairs={{38,0},{27,1},{40,2},{29,3},{42,4},{31,5},{44,6},{33,7},{46,8},{35... | collective-permute-start | bytes 208904 | tf_op jit(solution)/shard_map/ppermute | solution.py:41
  123.7 10.5 %collective-permute-start.21 = (bf16[2,136,128]{2,1,0:T(8,128)(2,1)S(1)}, bf16[2,136,128]{2,1,0:T(8,128)(2,1)S(1)}, u32[]{:S(2)}, u32[]{:S(2)}) collective-permute-start(bf16[2,136,128]{2,1,0:T(8,128)(2,1)S(1)} %shard_map.70), channel_id=1, source_target_pairs={{0,1},{1,0},{2,3},{3,2},{4,5},{5,4},{6,7},{7,6},{8,9},{9,8},{10,11... | collective-permute-start | bytes 208904 | tf_op jit(solution)/shard_map/ppermute | solution.py:46

commit v2 on v1

--- a/solution.py
+++ b/solution.py
@@ -84,44 +84,66 @@
 
 
 def gather_kernel(run_len, count, table_ref, own_lat, partner_lat, own_rot, partner_rot, *refs):
-    outs, sems = refs[:-1], refs[-1]
+    n = len(GROUPS)
+    keys_refs, rotary_refs, buffers = refs[:n], refs[n : 2 * n], refs[2 * n : 3 * n]
+    lat_sems, rot_sems = refs[3 * n :]
     entry = 2 * (run_len + 1)
     for k, (d, held) in enumerate(GROUPS):
-        keys_ref, rotary_ref = outs[2 * k], outs[2 * k + 1]
         for g, o in enumerate(held):
             request = request_at(table_ref, o + d, count)
             for which, (lat, rot) in enumerate(((own_lat, own_rot), (partner_lat, partner_rot))):
                 for j in range(run_len):
                     page = table_ref[2 + request * entry + which * (run_len + 1) + j]
                     slot = which * run_len + j
-                    for kind, (cache, to_ref) in enumerate(((lat, keys_ref), (rot, rotary_ref))):
+                    for cache, to_ref, sems in (
+                        (rot, buffers[k], rot_sems),
+                        (lat, keys_refs[k], lat_sems),
+                    ):
                         size = cache.shape[1]
                         pltpu.make_async_copy(
-                            cache.at[page], to_ref.at[g, pl.ds(slot * size, size)], sems.at[2 * k + kind]
+                            cache.at[page], to_ref.at[g, pl.ds(slot * size, size)], sems.at[k]
                         ).start()
-    for k, ref in enumerate(outs):
-        pltpu.make_async_copy(ref, ref, sems.at[k]).wait()
+
+    tokens = rotary_refs[0].shape[1]
+    row_of = lax.broadcasted_iota(jnp.int32, (tokens, tokens // 2), 0) // 2
+    row_in = lax.broadcasted_iota(jnp.int32, (tokens, tokens // 2), 1)
+    spread = jnp.where(row_of == row_in, 1.0, 0.0).astype(jnp.bfloat16)
+    token_odd = lax.broadcasted_iota(jnp.int32, (tokens, LANES), 0) % 2
+    kept = token_odd == lax.broadcasted_iota(jnp.int32, (tokens, LANES), 1) // ROPE
+    for k, (ref, buffer) in enumerate(zip(rotary_refs, buffers)):
+        pltpu.make_async_copy(buffer, buffer, rot_sems.at[k]).wait()
+        for g in range(ref.shape[0]):
+            rows = jnp.dot(spread, buffer[g], preferred_element_type=jnp.float32)
+            ref[g] = jnp.where(kept, rows, 0.0).astype(ref.dtype)
+    for k, ref in enumerate(keys_refs):
+        pltpu.make_async_copy(ref, ref, lat_sems.at[k]).wait()
 
 
 def gather_pages(table, caches, run_len, count):
-    shapes = []
-    for _, held in GROUPS:
-        for cache in caches[::2]:
-            size, lanes = cache.shape[1:]
-            shapes.append(jax.ShapeDtypeStruct((len(held), 2 * run_len * size, lanes), jnp.bfloat16))
+    page_len, width = caches[0].shape[1:]
+    rows = caches[2].shape[1]
+    pages = 2 * run_len
+
+    def shapes(size, lanes):
+        return [(len(held), pages * size, lanes) for _, held in GROUPS]
+
+    made = shapes(page_len, width) + shapes(page_len, LANES)
     outs = pl.pallas_call(
         lambda *refs: gather_kernel(run_len, count, *refs),
-        out_shape=shapes,
+        out_shape=[jax.ShapeDtypeStruct(shape, jnp.bfloat16) for shape in made],
         in_specs=[pl.BlockSpec(memory_space=pltpu.SMEM)] + [HBM] * 4,
-        out_specs=[VMEM] * len(shapes),
-        scratch_shapes=[pltpu.SemaphoreType.DMA((len(shapes),))],
+        out_specs=[VMEM] * len(made),
+        scratch_shapes=[pltpu.VMEM(shape, jnp.bfloat16) for shape in shapes(rows, LANES)]
+        + [pltpu.SemaphoreType.DMA((len(GROUPS),))] * 2,
         compiler_params=pltpu.CompilerParams(vmem_limit_bytes=34 << 20),
         cost_estimate=pl.CostEstimate(
-            flops=1 << 32, bytes_accessed=2 * sum(s.size * 2 for s in shapes), transcendentals=0
+            flops=1 << 32,
+            bytes_accessed=4 * sum(math.prod(shape) for shape in made),
+            transcendentals=0,
         ),
         name="gather_pages",
     )(table, *caches)
-    return [(outs[2 * k], outs[2 * k + 1]) for k in range(len(GROUPS))]
+    return list(zip(outs[: len(GROUPS)], outs[len(GROUPS) :]))
 
 
 def attention_kernel(offsets, run_len, count, table_ref, q_ref, keys_ref, rotary_ref, out_ref):
@@ -134,12 +156,6 @@
     lane = lax.broadcasted_iota(jnp.int32, (heads, LANES), 1)
     rope_lane = lax.broadcasted_iota(jnp.int32, (ROPE_ROWS, LANES), 1)
     column = lax.broadcasted_iota(jnp.int32, (heads, tokens), 1)
-    row_of = lax.broadcasted_iota(jnp.int32, (tokens, tokens // 2), 0) // 2
-    row_in = lax.broadcasted_iota(jnp.int32, (tokens, tokens // 2), 1)
-    spread = jnp.where(row_of == row_in, 1.0, 0.0).astype(jnp.bfloat16)
-    token_odd = lax.broadcasted_iota(jnp.int32, (tokens, LANES), 0) % 2
-    half_of = lax.broadcasted_iota(jnp.int32, (tokens, LANES), 1) // ROPE
-    kept = token_odd == half_of
     over_width = (((1,), (1,)), ((), ()))
     each = range(len(offsets))
     scores, lives = [], []
@@ -153,11 +169,9 @@
             [jnp.where(rope_lane < ROPE, rope, other), jnp.where(rope_lane < ROPE, other, rope)],
             axis=0,
         ).astype(jnp.bfloat16)
-        rotary = jnp.dot(spread, rotary_ref[g], preferred_element_type=jnp.float32)
-        rotary = jnp.where(kept, rotary, 0.0).astype(jnp.bfloat16)
         score = lax.dot_general(query, keys_ref[g], over_width, preferred_element_type=jnp.float32)
         score = score + lax.dot_general(
-            query_rope, rotary, over_width, preferred_element_type=jnp.float32
+            query_rope, rotary_ref[g], over_width, preferred_element_type=jnp.float32
         )
         request = request_at(table_ref, offsets[g], count)
         own_live = table_ref[2 + request * entry + run_len]
@@ -316,17 +330,15 @@
     six, thirteen, _ = lax.optimization_barrier((six, thirteen, pages[-1][1]))
     crossing = swapped(joined([six, thirteen], ((0, 1), (1, 1))))
     where = {0: (0, 0), 6: (1, 0), 13: (2, 0), -6: (3, 0), -13: (3, 1)}
-    far = joined([block, six, thirteen, crossing], [where[o] for o in FAR])
-
-    near = {d: shift_from(far, d) for d in (2, -2, 1, -1)}
-    for d in (3, -3):
-        step = d // 3
-        onward = joined([near[2 * step]], [(0, FAR.index(o)) for o in NEAR[d]])
-        near[d] = shift_from(onward, step)
+    lists = [held for held in dict.fromkeys(held for _, held in GROUPS)]
+    fars = joined([block, six, thirteen, crossing], *[[where[o] for o in held] for held in lists])
+    fars = dict(zip(lists, fars))
+
+    near = {d: shift_from(fars[held], d) for d, held in NEAR.items()}
     partials, sources = [], []
     for (d, held), group_pages in zip(GROUPS, pages):
         offsets = tuple(o + d for o in held)
-        queries = near[d] if d else far
+        queries = near[d] if d else fars[held]
         partial = attention(offsets, table, queries, group_pages, run_len, seq_count)
         partials.append(shift_from(partial, -d) if d else partial)
         sources.append(held)

time: 136 us -> 134 us (0.985)
  the two profiles are of different devices: /device:TPU:38 before, /device:TPU:37 now
where the time goes in v2:
time: 134 us
  starting transfers between devices  74.9 us (56%)
  waiting for transfers between devices  31.9 us (24%)
  Pallas kernels  20.3 us (15%)
  local copies, waits for them, and re-layouts  5.45 us (4%)
    ppermute x16, starting transfers between devices, shift_from(): return lax.ppermute(array, ('seq', 'head'), pairs)  44.5 us
    ppermute x6, starting transfers between devices, swapped(): lax.ppermute(array, 'head', [(c, cores - 1 - c) for c in range(cores)])  30.4 us
    ppermute x16, waiting for transfers between devices, shift_from(): return lax.ppermute(array, ('seq', 'head'), pairs)  28 us
    pallas_call x7, Pallas kernels, attention(): pl.pallas_call(lambda *refs: attention_kernel(offsets, run_len, count, *r...  11.8 us
    pallas_call x1, Pallas kernels, gather_pages(): pl.pallas_call(lambda *refs: gather_kernel(run_len, count, *refs), out_sh...  7.06 us
    ppermute x6, waiting for transfers between devices, swapped(): lax.ppermute(array, 'head', [(c, cores - 1 - c) for c in range(cores)])  3.93 us
  transfers between devices with their start and end apart: 22, of which 11 were waited for; matrix products, arithmetic and copies ran while one was open for 4% of the time, Pallas kernels for 14%

profile of v2, /device:TPU:37, one launch (start us, length us, event | category | flops | bytes accessed | tf_op | source)
XLA Modules:
  0.0 133.8 jit_solution(16824584544233803324)
XLA Ops:
  1.7 20.4 %collective-permute-start = (bf16[1,144,128]{2,1,0:T(8,128)(2,1)S(1)}, bf16[1,144,128]{2,1,0:T(8,128)(2,1)S(1)}, u32[]{:S(2)}, u32[]{:S(2)}) collective-permute-start(bf16[1,144,128]{2,1,0:T(8,128)(2,1)S(1)} %pack.1.refs_0_), channel_id=1, source_target_pairs={{0,1},{1,0},{2,3},{3,2},{4,5},{5,4},{6,7},{7,6},{8,9},{9,8},{10,11... | collective-permute-start | bytes 110600 | tf_op jit(solution)/shard_map/ppermute | solution.py:46
  23.5 13.3 %collective-permute-start.3 = (bf16[2,144,128]{2,1,0:T(8,128)(2,1)S(1)}, bf16[2,144,128]{2,1,0:T(8,128)(2,1)S(1)}, u32[]{:S(2)}, u32[]{:S(2)}) collective-permute-start(bf16[2,144,128]{2,1,0:T(8,128)(2,1)S(1)} %shard_map.64), channel_id=1, source_target_pairs={{26,0},{39,1},{28,2},{41,3},{30,4},{43,5},{32,6},{45,7},{34,8},{47... | collective-permute-start | bytes 221192 | tf_op jit(solution)/shard_map/ppermute | solution.py:41
  41.7 7.1 %gather_pages.1 = (bf16[5,384,512]{2,1,0:T(8,128)(2,1)S(1)}, bf16[5,384,512]{2,1,0:T(8,128)(2,1)S(1)}, bf16[5,384,512]{2,1,0:T(8,128)(2,1)S(1)}, bf16[5,384,512]...) custom-call(s32[258]{0:T(512)S(1)} %pad_add_fusion.1.refs_0_, ...), custom_call_target="tpu_custom_call" | custom-call | flops 4294967296 | bytes 31457280 | tf_op jit(solution)/shard_map/gather_pages/pallas_call | solution.py:131
  49.4 3.5 %collective-permute-start.5 = (bf16[2,144,128]{2,1,0:T(8,128)(2,1)S(1)}, bf16[2,144,128]{2,1,0:T(8,128)(2,1)S(1)}, u32[]{:S(2)}, u32[]{:S(2)}) collective-permute-start(bf16[2,144,128]{2,1,0:T(8,128)(2,1)S(1)} %shard_map.65), channel_id=1, source_target_pairs={{0,1},{1,0},{2,3},{3,2},{4,5},{5,4},{6,7},{7,6},{8,9},{9,8},{10,11... | collective-permute-start | bytes 221192 | tf_op jit(solution)/shard_map/ppermute | solution.py:46
  53.9 4.6 %collective-permute-start.16 = (bf16[3,144,128]{2,1,0:T(8,128)(2,1)S(1)}, bf16[3,144,128]{2,1,0:T(8,128)(2,1)S(1)}, u32[]{:S(2)}, u32[]{:S(2)}) collective-permute-start(bf16[3,144,128]{2,1,0:T(8,128)(2,1)S(1)} %get-tuple-element.56), channel_id=1, source_target_pairs={{58,0},{7,1},{60,2},{9,3},{62,4},{11,5},{0,6},{13,7},{2,8},{15,9},... | collective-permute-start | bytes 331784 | tf_op jit(solution)/shard_map/ppermute | solution.py:41
  58.5 1.5 %collective-permute-start.10 = (bf16[5,144,128]{2,1,0:T(8,128)(2,1)S(1)}, bf16[5,144,128]{2,1,0:T(8,128)(2,1)S(1)}, u32[]{:S(2)}, u32[]{:S(2)}) collective-permute-start(bf16[5,144,128]{2,1,0:T(8,128)(2,1)S(1)} %get-tuple-element.42.refs_1_), channel_id=1, source_target_pairs={{2,0},{63,1},{4,2},{1,3},{6,4},{3,5},{8,6},{5,7},{10,8},{7,9},{12,... | collective-permute-start | bytes 552968 | tf_op jit(solution)/shard_map/ppermute | solution.py:41
  59.9 2.4 %collective-permute-start.6 = (bf16[5,144,128]{2,1,0:T(8,128)(2,1)S(1)}, bf16[5,144,128]{2,1,0:T(8,128)(2,1)S(1)}, u32[]{:S(2)}, u32[]{:S(2)}) collective-permute-start(bf16[5,144,128]{2,1,0:T(8,128)(2,1)S(1)} %get-tuple-element.42.refs_1_), channel_id=1, source_target_pairs={{4,0},{61,1},{6,2},{63,3},{8,4},{1,5},{10,6},{3,7},{12,8},{5,9},{1... | collective-permute-start | bytes 552968 | tf_op jit(solution)/shard_map/ppermute | solution.py:41
  62.8 2.0 %collective-permute-start.14 = (bf16[4,144,128]{2,1,0:T(8,128)(2,1)S(1)}, bf16[4,144,128]{2,1,0:T(8,128)(2,1)S(1)}, u32[]{:S(2)}, u32[]{:S(2)}) collective-permute-start(bf16[4,144,128]{2,1,0:T(8,128)(2,1)S(1)} %get-tuple-element.53), channel_id=1, source_target_pairs={{6,0},{59,1},{8,2},{61,3},{10,4},{63,5},{12,6},{1,7},{14,8},{3,9},... | collective-permute-start | bytes 442376 | tf_op jit(solution)/shard_map/ppermute | solution.py:41
  66.2 4.6 %collective-permute-done.12.refs_1_ = bf16[5,144,128]{2,1,0:T(8,128)(2,1)S(1)} collective-permute-done((bf16[5,144,128]{2,1,0:T(8,128)(2,1)S(1)}, bf16[5,144,128]{2,1,0:T(8,128)(2,1)S(1)}, u32[]{:S(2)}, u32[]{:S(2)}) %collective-permute-start.12) | collective-permute-done | bytes 184352 | tf_op jit(solution)/shard_map/ppermute | solution.py:41
  72.0 1.8 %attention.11 = bf16[5,136,128]{2,1,0:T(8,128)(2,1)S(1)} custom-call(s32[258]{0:T(512)S(1)} %pad_add_fusion.1.refs_0_, bf16[5,144,128]{2,1,0:T(8,128)(2,1)S(1)} %collective-permute-done.12.refs_1_, bf16[5,384,512]{2,1,0:T(8,128)(2,1)S(1)} %get-tuple-element.51.refs_2_, bf16[5,384,128]{2,1,0:T(8,128)(2,1)S(1)} %get-tuple-element.52.refs_3_), custom_call_target="tpu_custom_call" | custom-call | flops 141557760 | bytes 2457600 | tf_op jit(solution)/shard_map/attention/pallas_call | solution.py:205
  74.1 1.8 %attention.10 = bf16[5,136,128]{2,1,0:T(8,128)(2,1)S(1)} custom-call(s32[258]{0:T(512)S(1)} %pad_add_fusion.1.refs_0_, bf16[5,144,128]{2,1,0:T(8,128)(2,1)S(1)} %collective-permute-done.10.refs_1_, bf16[5,384,512]{2,1,0:T(8,128)(2,1)S(1)} %get-tuple-element.49.refs_2_, bf16[5,384,128]{2,1,0:T(8,128)(2,1)S(1)} %get-tuple-element.50.refs_3_), custom_call_target="tpu_custom_call" | custom-call | flops 141557760 | bytes 2457600 | tf_op jit(solution)/shard_map/attention/pallas_call | solution.py:205
  75.9 1.8 %collective-permute-done.8.refs_1_ = bf16[5,144,128]{2,1,0:T(8,128)(2,1)S(1)} collective-permute-done((bf16[5,144,128]{2,1,0:T(8,128)(2,1)S(1)}, bf16[5,144,128]{2,1,0:T(8,128)(2,1)S(1)}, u32[]{:S(2)}, u32[]{:S(2)}) %collective-permute-start.8) | collective-permute-done | bytes 184352 | tf_op jit(solution)/shard_map/ppermute | solution.py:41
  78.5 1.8 %attention.9 = bf16[5,136,128]{2,1,0:T(8,128)(2,1)S(1)} custom-call(s32[258]{0:T(512)S(1)} %pad_add_fusion.1.refs_0_, bf16[5,144,128]{2,1,0:T(8,128)(2,1)S(1)} %collective-permute-done.8.refs_1_, bf16[5,384,512]{2,1,0:T(8,128)(2,1)S(1)} %get-tuple-element.47.refs_2_, bf16[5,384,128]{2,1,0:T(8,128)(2,1)S(1)} %get-tuple-element.48.refs_3_), custom_call_target="tpu_custom_call" | custom-call | flops 141557760 | bytes 2457600 | tf_op jit(solution)/shard_map/attention/pallas_call | solution.py:205
  80.2 2.6 %collective-permute-start.9 = (bf16[5,136,128]{2,1,0:T(8,128)(2,1)S(1)}, bf16[5,136,128]{2,1,0:T(8,128)(2,1)S(1)}, u32[]{:S(2)}, u32[]{:S(2)}) collective-permute-start(bf16[5,136,128]{2,1,0:T(8,128)(2,1)S(1)} %attention.9), channel_id=1, source_target_pairs={{4,0},{61,1},{6,2},{63,3},{8,4},{1,5},{10,6},{3,7},{12,8},{5,9},{1... | collective-permute-start | bytes 522248 | tf_op jit(solution)/shard_map/ppermute | solution.py:41
  82.8 1.8 %attention.8 = bf16[5,136,128]{2,1,0:T(8,128)(2,1)S(1)} custom-call(s32[258]{0:T(512)S(1)} %pad_add_fusion.1.refs_0_, bf16[5,144,128]{2,1,0:T(8,128)(2,1)S(1)} %collective-permute-done.6.refs_1_, bf16[5,384,512]{2,1,0:T(8,128)(2,1)S(1)} %get-tuple-element.45.refs_2_, bf16[5,384,128]{2,1,0:T(8,128)(2,1)S(1)} %get-tuple-element.46.refs_3_), custom_call_target="tpu_custom_call" | custom-call | flops 141557760 | bytes 2457600 | tf_op jit(solution)/shard_map/attention/pallas_call | solution.py:205
  85.8 1.6 %attention.12 = bf16[4,136,128]{2,1,0:T(8,128)(2,1)S(1)} custom-call(s32[258]{0:T(512)S(1)} %pad_add_fusion.1.refs_0_, bf16[4,144,128]{2,1,0:T(8,128)(2,1)S(1)} %collective-permute-done.14.refs_1_, bf16[4,384,512]{2,1,0:T(8,128)(2,1)S(1)} %get-tuple-element.54.refs_2_, bf16[4,384,128]{2,1,0:T(8,128)(2,1)S(1)} %get-tuple-element.55.refs_3_), custom_call_target="tpu_custom_call" | custom-call | flops 113246208 | bytes 1966080 | tf_op jit(solution)/shard_map/attention/pallas_call | solution.py:205
  87.4 3.2 %collective-permute-start.15 = (bf16[4,136,128]{2,1,0:T(8,128)(2,1)S(1)}, bf16[4,136,128]{2,1,0:T(8,128)(2,1)S(1)}, u32[]{:S(2)}, u32[]{:S(2)}) collective-permute-start(bf16[4,136,128]{2,1,0:T(8,128)(2,1)S(1)} %attention.12), channel_id=1, source_target_pairs={{58,0},{7,1},{60,2},{9,3},{62,4},{11,5},{0,6},{13,7},{2,8},{15,9},... | collective-permute-start | bytes 417800 | tf_op jit(solution)/shard_map/ppermute | solution.py:41
  90.6 1.8 %attention.7.refs_0_ = bf16[5,136,128]{2,1,0:T(8,128)(2,1)S(1)} custom-call(s32[258]{0:T(512)S(1)} %pad_add_fusion.1.refs_0_, bf16[5,144,128]{2,1,0:T(8,128)(2,1)S(1)} %get-tuple-element.42.refs_1_, bf16[5,384,512]{2,1,0:T(8,128)(2,1)S(1)} %get-tuple-element.43.refs_2_, bf16[5,384,128]{2,1,0:T(8,128)(2,1)S(1)} %get-tuple-element.44.refs_3_), custom_call_target="tpu_custom_call" | custom-call | flops 141557760 | bytes 2457600 | tf_op jit(solution)/shard_map/attention/pallas_call | solution.py:205
  92.4 2.5 %collective-permute-done.15.refs_5_ = bf16[4,136,128]{2,1,0:T(8,128)(2,1)S(1)} collective-permute-done((bf16[4,136,128]{2,1,0:T(8,128)(2,1)S(1)}, bf16[4,136,128]{2,1,0:T(8,128)(2,1)S(1)}, u32[]{:S(2)}, u32[]{:S(2)}) %collective-permute-start.15) | collective-permute-done | bytes 139296 | tf_op jit(solution)/shard_map/ppermute | solution.py:41
  94.9 1.6 %collective-permute-done.7.refs_1_ = bf16[5,136,128]{2,1,0:T(8,128)(2,1)S(1)} collective-permute-done((bf16[5,136,128]{2,1,0:T(8,128)(2,1)S(1)}, bf16[5,136,128]{2,1,0:T(8,128)(2,1)S(1)}, u32[]{:S(2)}, u32[]{:S(2)}) %collective-permute-start.7) | collective-permute-done | bytes 174112 | tf_op jit(solution)/shard_map/ppermute | solution.py:41
  96.9 6.0 %collective-permute-start.18 = (bf16[2,136,128]{2,1,0:T(8,128)(2,1)S(1)}, bf16[2,136,128]{2,1,0:T(8,128)(2,1)S(1)}, u32[]{:S(2)}, u32[]{:S(2)}) collective-permute-start(bf16[2,136,128]{2,1,0:T(8,128)(2,1)S(1)} %get-tuple-element.60), channel_id=1, source_target_pairs={{0,1},{1,0},{2,3},{3,2},{4,5},{5,4},{6,7},{7,6},{8,9},{9,8},{10,11... | collective-permute-start | bytes 208904 | tf_op jit(solution)/shard_map/ppermute | solution.py:46
  103.8 5.6 %collective-permute-start.19 = (bf16[2,136,128]{2,1,0:T(8,128)(2,1)S(1)}, bf16[2,136,128]{2,1,0:T(8,128)(2,1)S(1)}, u32[]{:S(2)}, u32[]{:S(2)}) collective-permute-start(bf16[2,136,128]{2,1,0:T(8,128)(2,1)S(1)} %get-tuple-element.61), channel_id=1, source_target_pairs={{52,0},{13,1},{54,2},{15,3},{56,4},{17,5},{58,6},{19,7},{60,8},{21... | collective-permute-start | bytes 208904 | tf_op jit(solution)/shard_map/ppermute | solution.py:41
  109.4 6.0 %collective-permute-start.20 = (bf16[2,136,128]{2,1,0:T(8,128)(2,1)S(1)}, bf16[2,136,128]{2,1,0:T(8,128)(2,1)S(1)}, u32[]{:S(2)}, u32[]{:S(2)}) collective-permute-start(bf16[2,136,128]{2,1,0:T(8,128)(2,1)S(1)} %get-tuple-element.62), channel_id=1, source_target_pairs={{38,0},{27,1},{40,2},{29,3},{42,4},{31,5},{44,6},{33,7},{46,8},{35... | collective-permute-start | bytes 208904 | tf_op jit(solution)/shard_map/ppermute | solution.py:41
  115.3 16.4 %collective-permute-done.20.refs_1_.refs_2_ = bf16[2,136,128]{2,1,0:T(8,128)(2,1)S(1)} collective-permute-done((bf16[2,136,128]{2,1,0:T(8,128)(2,1)S(1)}, bf16[2,136,128]{2,1,0:T(8,128)(2,1)S(1)}, u32[]{:S(2)}, u32[]{:S(2)}) %collective-permute-start.20) | collective-permute-done | bytes 69664 | tf_op jit(solution)/shard_map/ppermute | solution.py:41
  (57 shorter events, 18.4 us)
Async XLA Ops:
  1.0 0.8 copy-start
  1.7 21.3 %collective-permute-start = (bf16[1,144,128]{2,1,0:T(8,128)(2,1)S(1)}, bf16[1,144,128]{2,1,0:T(8,128)(2,1)S(1)}, u32[]{:S(2)}, u32[]{:S(2)}) collective-permute-start(bf16[1,144,128]{2,1,0:T(8,128)(2,1)S(1)} %pack.1.refs_0_), channel_id=1, source_target_pairs={{0,1},{1,0},{2,3},{3,2},{4,5},{5,4},{6,7},{7,6},{8,9},{9,8},{10,11... | collective-permute-start | bytes 110600 | tf_op jit(solution)/shard_map/ppermute | solution.py:46
  23.0 18.7 %collective-permute-start.4 = (bf16[96,64,512]{2,1,0:T(8,128)(2,1)}, bf16[96,64,512]{2,1,0:T(8,128)(2,1)}, u32[]{:S(2)}, u32[]{:S(2)}) collective-permute-start(bf16[96,64,512]{2,1,0:T(8,128)(2,1)} %refs_1_.1), channel_id=1, source_target_pairs={{0,1},{1,0},{2,3},{3,2},{4,5},{5,4},{6,7},{7,6},{8,9},{9,8},{10,11... | collective-permute-start | bytes 18874376 | tf_op jit(solution)/shard_map/ppermute | solution.py:46
  23.4 13.5 %collective-permute-start.1 = (bf16[96,4096]{1,0:T(8,128)(2,1)}, bf16[96,4096]{1,0:T(8,128)(2,1)S(1)}, u32[]{:S(2)}, u32[]{:S(2)}) collective-permute-start(bf16[96,4096]{1,0:T(8,128)(2,1)} %param.9), channel_id=1, source_target_pairs={{0,1},{1,0},{2,3},{3,2},{4,5},{5,4},{6,7},{7,6},{8,9},{9,8},{10,11... | collective-permute-start | bytes 2359304 | tf_op jit(solution)/shard_map/ppermute | solution.py:46
  23.5 25.2 %collective-permute-start.2 = (bf16[2,144,128]{2,1,0:T(8,128)(2,1)S(1)}, bf16[2,144,128]{2,1,0:T(8,128)(2,1)S(1)}, u32[]{:S(2)}, u32[]{:S(2)}) collective-permute-start(bf16[2,144,128]{2,1,0:T(8,128)(2,1)S(1)} %shard_map.64), channel_id=1, source_target_pairs={{12,0},{53,1},{14,2},{55,3},{16,4},{57,5},{18,6},{59,7},{20,8},{61... | collective-permute-start | bytes 221192 | tf_op jit(solution)/shard_map/ppermute | solution.py:41
  23.5 25.8 %collective-permute-start.3 = (bf16[2,144,128]{2,1,0:T(8,128)(2,1)S(1)}, bf16[2,144,128]{2,1,0:T(8,128)(2,1)S(1)}, u32[]{:S(2)}, u32[]{:S(2)}) collective-permute-start(bf16[2,144,128]{2,1,0:T(8,128)(2,1)S(1)} %shard_map.64), channel_id=1, source_target_pairs={{26,0},{39,1},{28,2},{41,3},{30,4},{43,5},{32,6},{45,7},{34,8},{47... | collective-permute-start | bytes 221192 | tf_op jit(solution)/shard_map/ppermute | solution.py:41
  49.4 4.4 %collective-permute-start.5 = (bf16[2,144,128]{2,1,0:T(8,128)(2,1)S(1)}, bf16[2,144,128]{2,1,0:T(8,128)(2,1)S(1)}, u32[]{:S(2)}, u32[]{:S(2)}) collective-permute-start(bf16[2,144,128]{2,1,0:T(8,128)(2,1)S(1)} %shard_map.65), channel_id=1, source_target_pairs={{0,1},{1,0},{2,3},{3,2},{4,5},{5,4},{6,7},{7,6},{8,9},{9,8},{10,11... | collective-permute-start | bytes 221192 | tf_op jit(solution)/shard_map/ppermute | solution.py:46
  53.9 8.9 %collective-permute-start.16 = (bf16[3,144,128]{2,1,0:T(8,128)(2,1)S(1)}, bf16[3,144,128]{2,1,0:T(8,128)(2,1)S(1)}, u32[]{:S(2)}, u32[]{:S(2)}) collective-permute-start(bf16[3,144,128]{2,1,0:T(8,128)(2,1)S(1)} %get-tuple-element.56), channel_id=1, source_target_pairs={{58,0},{7,1},{60,2},{9,3},{62,4},{11,5},{0,6},{13,7},{2,8},{15,9},... | collective-permute-start | bytes 331784 | tf_op jit(solution)/shard_map/ppermute | solution.py:41
  58.5 12.4 %collective-permute-start.12 = (bf16[5,144,128]{2,1,0:T(8,128)(2,1)S(1)}, bf16[5,144,128]{2,1,0:T(8,128)(2,1)S(1)}, u32[]{:S(2)}, u32[]{:S(2)}) collective-permute-start(bf16[5,144,128]{2,1,0:T(8,128)(2,1)S(1)} %get-tuple-element.42.refs_1_), channel_id=1, source_target_pairs={{62,0},{3,1},{0,2},{5,3},{2,4},{7,5},{4,6},{9,7},{6,8},{11,9},{8,1... | collective-permute-start | bytes 552968 | tf_op jit(solution)/shard_map/ppermute | solution.py:41
  58.5 15.3 %collective-permute-start.10 = (bf16[5,144,128]{2,1,0:T(8,128)(2,1)S(1)}, bf16[5,144,128]{2,1,0:T(8,128)(2,1)S(1)}, u32[]{:S(2)}, u32[]{:S(2)}) collective-permute-start(bf16[5,144,128]{2,1,0:T(8,128)(2,1)S(1)} %get-tuple-element.42.refs_1_), channel_id=1, source_target_pairs={{2,0},{63,1},{4,2},{1,3},{6,4},{3,5},{8,6},{5,7},{10,8},{7,9},{12,... | collective-permute-start | bytes 552968 | tf_op jit(solution)/shard_map/ppermute | solution.py:41
  59.9 17.8 %collective-permute-start.8 = (bf16[5,144,128]{2,1,0:T(8,128)(2,1)S(1)}, bf16[5,144,128]{2,1,0:T(8,128)(2,1)S(1)}, u32[]{:S(2)}, u32[]{:S(2)}) collective-permute-start(bf16[5,144,128]{2,1,0:T(8,128)(2,1)S(1)} %get-tuple-element.42.refs_1_), channel_id=1, source_target_pairs={{60,0},{5,1},{62,2},{7,3},{0,4},{9,5},{2,6},{11,7},{4,8},{13,9},{6... | collective-permute-start | bytes 552968 | tf_op jit(solution)/shard_map/ppermute | solution.py:41
  59.9 20.3 %collective-permute-start.6 = (bf16[5,144,128]{2,1,0:T(8,128)(2,1)S(1)}, bf16[5,144,128]{2,1,0:T(8,128)(2,1)S(1)}, u32[]{:S(2)}, u32[]{:S(2)}) collective-permute-start(bf16[5,144,128]{2,1,0:T(8,128)(2,1)S(1)} %get-tuple-element.42.refs_1_), channel_id=1, source_target_pairs={{4,0},{61,1},{6,2},{63,3},{8,4},{1,5},{10,6},{3,7},{12,8},{5,9},{1... | collective-permute-start | bytes 552968 | tf_op jit(solution)/shard_map/ppermute | solution.py:41
  62.8 21.8 %collective-permute-start.14 = (bf16[4,144,128]{2,1,0:T(8,128)(2,1)S(1)}, bf16[4,144,128]{2,1,0:T(8,128)(2,1)S(1)}, u32[]{:S(2)}, u32[]{:S(2)}) collective-permute-start(bf16[4,144,128]{2,1,0:T(8,128)(2,1)S(1)} %get-tuple-element.53), channel_id=1, source_target_pairs={{6,0},{59,1},{8,2},{61,3},{10,4},{63,5},{12,6},{1,7},{14,8},{3,9},... | collective-permute-start | bytes 442376 | tf_op jit(solution)/shard_map/ppermute | solution.py:41
  70.9 16.6 %collective-permute-start.17 = (bf16[3,136,128]{2,1,0:T(8,128)(2,1)S(1)}, bf16[3,136,128]{2,1,0:T(8,128)(2,1)S(1)}, u32[]{:S(2)}, u32[]{:S(2)}) collective-permute-start(bf16[3,136,128]{2,1,0:T(8,128)(2,1)S(1)} %attention.13), channel_id=1, source_target_pairs={{6,0},{59,1},{8,2},{61,3},{10,4},{63,5},{12,6},{1,7},{14,8},{3,9},... | collective-permute-start | bytes 313352 | tf_op jit(solution)/shard_map/ppermute | solution.py:41
  73.8 21.1 %collective-permute-start.13 = (bf16[5,136,128]{2,1,0:T(8,128)(2,1)S(1)}, bf16[5,136,128]{2,1,0:T(8,128)(2,1)S(1)}, u32[]{:S(2)}, u32[]{:S(2)}) collective-permute-start(bf16[5,136,128]{2,1,0:T(8,128)(2,1)S(1)} %attention.11), channel_id=1, source_target_pairs={{2,0},{63,1},{4,2},{1,3},{6,4},{3,5},{8,6},{5,7},{10,8},{7,9},{12,... | collective-permute-start | bytes 522248 | tf_op jit(solution)/shard_map/ppermute | solution.py:41
  77.7 17.2 %collective-permute-start.11 = (bf16[5,136,128]{2,1,0:T(8,128)(2,1)S(1)}, bf16[5,136,128]{2,1,0:T(8,128)(2,1)S(1)}, u32[]{:S(2)}, u32[]{:S(2)}) collective-permute-start(bf16[5,136,128]{2,1,0:T(8,128)(2,1)S(1)} %attention.10), channel_id=1, source_target_pairs={{62,0},{3,1},{0,2},{5,3},{2,4},{7,5},{4,6},{9,7},{6,8},{11,9},{8,1... | collective-permute-start | bytes 522248 | tf_op jit(solution)/shard_map/ppermute | solution.py:41
  80.2 14.7 %collective-permute-start.9 = (bf16[5,136,128]{2,1,0:T(8,128)(2,1)S(1)}, bf16[5,136,128]{2,1,0:T(8,128)(2,1)S(1)}, u32[]{:S(2)}, u32[]{:S(2)}) collective-permute-start(bf16[5,136,128]{2,1,0:T(8,128)(2,1)S(1)} %attention.9), channel_id=1, source_target_pairs={{4,0},{61,1},{6,2},{63,3},{8,4},{1,5},{10,6},{3,7},{12,8},{5,9},{1... | collective-permute-start | bytes 522248 | tf_op jit(solution)/shard_map/ppermute | solution.py:41
  84.6 11.9 %collective-permute-start.7 = (bf16[5,136,128]{2,1,0:T(8,128)(2,1)S(1)}, bf16[5,136,128]{2,1,0:T(8,128)(2,1)S(1)}, u32[]{:S(2)}, u32[]{:S(2)}) collective-permute-start(bf16[5,136,128]{2,1,0:T(8,128)(2,1)S(1)} %attention.8), channel_id=1, source_target_pairs={{60,0},{5,1},{62,2},{7,3},{0,4},{9,5},{2,6},{11,7},{4,8},{13,9},{6... | collective-permute-start | bytes 522248 | tf_op jit(solution)/shard_map/ppermute | solution.py:41
  87.4 7.5 %collective-permute-start.15 = (bf16[4,136,128]{2,1,0:T(8,128)(2,1)S(1)}, bf16[4,136,128]{2,1,0:T(8,128)(2,1)S(1)}, u32[]{:S(2)}, u32[]{:S(2)}) collective-permute-start(bf16[4,136,128]{2,1,0:T(8,128)(2,1)S(1)} %attention.12), channel_id=1, source_target_pairs={{58,0},{7,1},{60,2},{9,3},{62,4},{11,5},{0,6},{13,7},{2,8},{15,9},... | collective-permute-start | bytes 417800 | tf_op jit(solution)/shard_map/ppermute | solution.py:41
  96.9 6.9 %collective-permute-start.18 = (bf16[2,136,128]{2,1,0:T(8,128)(2,1)S(1)}, bf16[2,136,128]{2,1,0:T(8,128)(2,1)S(1)}, u32[]{:S(2)}, u32[]{:S(2)}) collective-permute-start(bf16[2,136,128]{2,1,0:T(8,128)(2,1)S(1)} %get-tuple-element.60), channel_id=1, source_target_pairs={{0,1},{1,0},{2,3},{3,2},{4,5},{5,4},{6,7},{7,6},{8,9},{9,8},{10,11... | collective-permute-start | bytes 208904 | tf_op jit(solution)/shard_map/ppermute | solution.py:46
  103.8 11.5 %collective-permute-start.19 = (bf16[2,136,128]{2,1,0:T(8,128)(2,1)S(1)}, bf16[2,136,128]{2,1,0:T(8,128)(2,1)S(1)}, u32[]{:S(2)}, u32[]{:S(2)}) collective-permute-start(bf16[2,136,128]{2,1,0:T(8,128)(2,1)S(1)} %get-tuple-element.61), channel_id=1, source_target_pairs={{52,0},{13,1},{54,2},{15,3},{56,4},{17,5},{58,6},{19,7},{60,8},{21... | collective-permute-start | bytes 208904 | tf_op jit(solution)/shard_map/ppermute | solution.py:41
  109.4 22.4 %collective-permute-start.20 = (bf16[2,136,128]{2,1,0:T(8,128)(2,1)S(1)}, bf16[2,136,128]{2,1,0:T(8,128)(2,1)S(1)}, u32[]{:S(2)}, u32[]{:S(2)}) collective-permute-start(bf16[2,136,128]{2,1,0:T(8,128)(2,1)S(1)} %get-tuple-element.62), channel_id=1, source_target_pairs={{38,0},{27,1},{40,2},{29,3},{42,4},{31,5},{44,6},{33,7},{46,8},{35... | collective-permute-start | bytes 208904 | tf_op jit(solution)/shard_map/ppermute | solution.py:41
  131.7 1.3 collective-permute-start.21

commit v3 on v2

--- a/solution.py
+++ b/solution.py
@@ -17,12 +17,12 @@
 
 FAR = (0, 6, 13, -6, -13)
 NEAR = {
+    3: (0, 6, 13, -13),
+    -3: (0, 13, -6),
     2: FAR,
     -2: FAR,
     1: FAR,
     -1: FAR,
-    3: (0, 6, 13, -13),
-    -3: (0, 13, -6),
 }
 GROUPS = ((0, FAR),) + tuple(NEAR.items())
 
@@ -334,13 +334,17 @@
     fars = joined([block, six, thirteen, crossing], *[[where[o] for o in held] for held in lists])
     fars = dict(zip(lists, fars))
 
-    near = {d: shift_from(fars[held], d) for d, held in NEAR.items()}
+    near = {}
+    for d, held in NEAR.items():
+        near[d] = shift_from(fars[held], d)
     partials, sources = [], []
     for (d, held), group_pages in zip(GROUPS, pages):
         offsets = tuple(o + d for o in held)
         queries = near[d] if d else fars[held]
         partial = attention(offsets, table, queries, group_pages, run_len, seq_count)
-        partials.append(shift_from(partial, -d) if d else partial)
+        if d:
+            partial = shift_from(partial, -d)
+        partials.append(partial)
         sources.append(held)
 
     home, ahead, across = pl.pallas_call(

time: 134 us -> 134 us (level)
  no operation moved by 1% of the time
where the time goes in v3:
time: 134 us
  starting transfers between devices  74.9 us (56%)
  waiting for transfers between devices  31.8 us (24%)
  Pallas kernels  20.3 us (15%)
  local copies, waits for them, and re-layouts  5.45 us (4%)
    ppermute x16, starting transfers between devices, shift_from(): return lax.ppermute(array, ('seq', 'head'), pairs)  44.5 us
    ppermute x6, starting transfers between devices, swapped(): lax.ppermute(array, 'head', [(c, cores - 1 - c) for c in range(cores)])  30.4 us
    ppermute x16, waiting for transfers between devices, shift_from(): return lax.ppermute(array, ('seq', 'head'), pairs)  27.9 us
    pallas_call x7, Pallas kernels, attention(): pl.pallas_call(lambda *refs: attention_kernel(offsets, run_len, count, *r...  11.8 us
    pallas_call x1, Pallas kernels, gather_pages(): pl.pallas_call(lambda *refs: gather_kernel(run_len, count, *refs), out_sh...  7.07 us
    ppermute x6, waiting for transfers between devices, swapped(): lax.ppermute(array, 'head', [(c, cores - 1 - c) for c in range(cores)])  3.93 us
  transfers between devices with their start and end apart: 22, of which 11 were waited for; matrix products, arithmetic and copies ran while one was open for 4% of the time, Pallas kernels for 14%

profile of v3, /device:TPU:37, one launch (start us, length us, event | category | flops | bytes accessed | tf_op | source)
XLA Modules:
  0.0 133.7 jit_solution(4080977965210612709)
XLA Ops:
  1.7 20.4 %collective-permute-start = (bf16[1,144,128]{2,1,0:T(8,128)(2,1)S(1)}, bf16[1,144,128]{2,1,0:T(8,128)(2,1)S(1)}, u32[]{:S(2)}, u32[]{:S(2)}) collective-permute-start(bf16[1,144,128]{2,1,0:T(8,128)(2,1)S(1)} %pack.1.refs_0_), channel_id=1, source_target_pairs={{0,1},{1,0},{2,3},{3,2},{4,5},{5,4},{6,7},{7,6},{8,9},{9,8},{10,11... | collective-permute-start | bytes 110600 | tf_op jit(solution)/shard_map/ppermute | solution.py:46
  23.5 13.3 %collective-permute-start.3 = (bf16[2,144,128]{2,1,0:T(8,128)(2,1)S(1)}, bf16[2,144,128]{2,1,0:T(8,128)(2,1)S(1)}, u32[]{:S(2)}, u32[]{:S(2)}) collective-permute-start(bf16[2,144,128]{2,1,0:T(8,128)(2,1)S(1)} %shard_map.64), channel_id=1, source_target_pairs={{26,0},{39,1},{28,2},{41,3},{30,4},{43,5},{32,6},{45,7},{34,8},{47... | collective-permute-start | bytes 221192 | tf_op jit(solution)/shard_map/ppermute | solution.py:41
  41.7 7.1 %gather_pages.1 = (bf16[5,384,512]{2,1,0:T(8,128)(2,1)S(1)}, bf16[4,384,512]{2,1,0:T(8,128)(2,1)S(1)}, bf16[3,384,512]{2,1,0:T(8,128)(2,1)S(1)}, bf16[5,384,512]...) custom-call(s32[258]{0:T(512)S(1)} %pad_add_fusion.1.refs_0_, ...), custom_call_target="tpu_custom_call" | custom-call | flops 4294967296 | bytes 31457280 | tf_op jit(solution)/shard_map/gather_pages/pallas_call | solution.py:131
  49.4 3.5 %collective-permute-start.5 = (bf16[2,144,128]{2,1,0:T(8,128)(2,1)S(1)}, bf16[2,144,128]{2,1,0:T(8,128)(2,1)S(1)}, u32[]{:S(2)}, u32[]{:S(2)}) collective-permute-start(bf16[2,144,128]{2,1,0:T(8,128)(2,1)S(1)} %shard_map.65), channel_id=1, source_target_pairs={{0,1},{1,0},{2,3},{3,2},{4,5},{5,4},{6,7},{7,6},{8,9},{9,8},{10,11... | collective-permute-start | bytes 221192 | tf_op jit(solution)/shard_map/ppermute | solution.py:46
  53.9 4.6 %collective-permute-start.8 = (bf16[3,144,128]{2,1,0:T(8,128)(2,1)S(1)}, bf16[3,144,128]{2,1,0:T(8,128)(2,1)S(1)}, u32[]{:S(2)}, u32[]{:S(2)}) collective-permute-start(bf16[3,144,128]{2,1,0:T(8,128)(2,1)S(1)} %get-tuple-element.48), channel_id=1, source_target_pairs={{58,0},{7,1},{60,2},{9,3},{62,4},{11,5},{0,6},{13,7},{2,8},{15,9},... | collective-permute-start | bytes 331784 | tf_op jit(solution)/shard_map/ppermute | solution.py:41
  58.5 1.5 %collective-permute-start.14 = (bf16[5,144,128]{2,1,0:T(8,128)(2,1)S(1)}, bf16[5,144,128]{2,1,0:T(8,128)(2,1)S(1)}, u32[]{:S(2)}, u32[]{:S(2)}) collective-permute-start(bf16[5,144,128]{2,1,0:T(8,128)(2,1)S(1)} %get-tuple-element.42.refs_1_), channel_id=1, source_target_pairs={{2,0},{63,1},{4,2},{1,3},{6,4},{3,5},{8,6},{5,7},{10,8},{7,9},{12,... | collective-permute-start | bytes 552968 | tf_op jit(solution)/shard_map/ppermute | solution.py:41
  59.9 2.4 %collective-permute-start.10 = (bf16[5,144,128]{2,1,0:T(8,128)(2,1)S(1)}, bf16[5,144,128]{2,1,0:T(8,128)(2,1)S(1)}, u32[]{:S(2)}, u32[]{:S(2)}) collective-permute-start(bf16[5,144,128]{2,1,0:T(8,128)(2,1)S(1)} %get-tuple-element.42.refs_1_), channel_id=1, source_target_pairs={{4,0},{61,1},{6,2},{63,3},{8,4},{1,5},{10,6},{3,7},{12,8},{5,9},{1... | collective-permute-start | bytes 552968 | tf_op jit(solution)/shard_map/ppermute | solution.py:41
  62.8 2.0 %collective-permute-start.6 = (bf16[4,144,128]{2,1,0:T(8,128)(2,1)S(1)}, bf16[4,144,128]{2,1,0:T(8,128)(2,1)S(1)}, u32[]{:S(2)}, u32[]{:S(2)}) collective-permute-start(bf16[4,144,128]{2,1,0:T(8,128)(2,1)S(1)} %get-tuple-element.45), channel_id=1, source_target_pairs={{6,0},{59,1},{8,2},{61,3},{10,4},{63,5},{12,6},{1,7},{14,8},{3,9},... | collective-permute-start | bytes 442376 | tf_op jit(solution)/shard_map/ppermute | solution.py:41
  66.2 4.6 %collective-permute-done.16.refs_1_ = bf16[5,144,128]{2,1,0:T(8,128)(2,1)S(1)} collective-permute-done((bf16[5,144,128]{2,1,0:T(8,128)(2,1)S(1)}, bf16[5,144,128]{2,1,0:T(8,128)(2,1)S(1)}, u32[]{:S(2)}, u32[]{:S(2)}) %collective-permute-start.16) | collective-permute-done | bytes 184352 | tf_op jit(solution)/shard_map/ppermute | solution.py:41
  72.0 1.8 %attention.13 = bf16[5,136,128]{2,1,0:T(8,128)(2,1)S(1)} custom-call(s32[258]{0:T(512)S(1)} %pad_add_fusion.1.refs_0_, bf16[5,144,128]{2,1,0:T(8,128)(2,1)S(1)} %collective-permute-done.16.refs_1_, bf16[5,384,512]{2,1,0:T(8,128)(2,1)S(1)} %get-tuple-element.57.refs_2_, bf16[5,384,128]{2,1,0:T(8,128)(2,1)S(1)} %get-tuple-element.39.refs_3_), custom_call_target="tpu_custom_call" | custom-call | flops 141557760 | bytes 2457600 | tf_op jit(solution)/shard_map/attention/pallas_call | solution.py:205
  74.1 1.8 %attention.12 = bf16[5,136,128]{2,1,0:T(8,128)(2,1)S(1)} custom-call(s32[258]{0:T(512)S(1)} %pad_add_fusion.1.refs_0_, bf16[5,144,128]{2,1,0:T(8,128)(2,1)S(1)} %collective-permute-done.14.refs_1_, bf16[5,384,512]{2,1,0:T(8,128)(2,1)S(1)} %get-tuple-element.55.refs_2_, bf16[5,384,128]{2,1,0:T(8,128)(2,1)S(1)} %get-tuple-element.56.refs_3_), custom_call_target="tpu_custom_call" | custom-call | flops 141557760 | bytes 2457600 | tf_op jit(solution)/shard_map/attention/pallas_call | solution.py:205
  75.9 1.8 %collective-permute-done.12.refs_1_ = bf16[5,144,128]{2,1,0:T(8,128)(2,1)S(1)} collective-permute-done((bf16[5,144,128]{2,1,0:T(8,128)(2,1)S(1)}, bf16[5,144,128]{2,1,0:T(8,128)(2,1)S(1)}, u32[]{:S(2)}, u32[]{:S(2)}) %collective-permute-start.12) | collective-permute-done | bytes 184352 | tf_op jit(solution)/shard_map/ppermute | solution.py:41
  78.5 1.8 %attention.11 = bf16[5,136,128]{2,1,0:T(8,128)(2,1)S(1)} custom-call(s32[258]{0:T(512)S(1)} %pad_add_fusion.1.refs_0_, bf16[5,144,128]{2,1,0:T(8,128)(2,1)S(1)} %collective-permute-done.12.refs_1_, bf16[5,384,512]{2,1,0:T(8,128)(2,1)S(1)} %get-tuple-element.53.refs_2_, bf16[5,384,128]{2,1,0:T(8,128)(2,1)S(1)} %get-tuple-element.54.refs_3_), custom_call_target="tpu_custom_call" | custom-call | flops 141557760 | bytes 2457600 | tf_op jit(solution)/shard_map/attention/pallas_call | solution.py:205
  80.2 2.6 %collective-permute-start.13 = (bf16[5,136,128]{2,1,0:T(8,128)(2,1)S(1)}, bf16[5,136,128]{2,1,0:T(8,128)(2,1)S(1)}, u32[]{:S(2)}, u32[]{:S(2)}) collective-permute-start(bf16[5,136,128]{2,1,0:T(8,128)(2,1)S(1)} %attention.11), channel_id=1, source_target_pairs={{4,0},{61,1},{6,2},{63,3},{8,4},{1,5},{10,6},{3,7},{12,8},{5,9},{1... | collective-permute-start | bytes 522248 | tf_op jit(solution)/shard_map/ppermute | solution.py:41
  82.8 1.8 %attention.10 = bf16[5,136,128]{2,1,0:T(8,128)(2,1)S(1)} custom-call(s32[258]{0:T(512)S(1)} %pad_add_fusion.1.refs_0_, bf16[5,144,128]{2,1,0:T(8,128)(2,1)S(1)} %collective-permute-done.10.refs_1_, bf16[5,384,512]{2,1,0:T(8,128)(2,1)S(1)} %get-tuple-element.51.refs_2_, bf16[5,384,128]{2,1,0:T(8,128)(2,1)S(1)} %get-tuple-element.52.refs_3_), custom_call_target="tpu_custom_call" | custom-call | flops 141557760 | bytes 2457600 | tf_op jit(solution)/shard_map/attention/pallas_call | solution.py:205
  85.8 1.6 %attention.8 = bf16[4,136,128]{2,1,0:T(8,128)(2,1)S(1)} custom-call(s32[258]{0:T(512)S(1)} %pad_add_fusion.1.refs_0_, bf16[4,144,128]{2,1,0:T(8,128)(2,1)S(1)} %collective-permute-done.6.refs_1_, bf16[4,384,512]{2,1,0:T(8,128)(2,1)S(1)} %get-tuple-element.46.refs_2_, bf16[4,384,128]{2,1,0:T(8,128)(2,1)S(1)} %get-tuple-element.47.refs_3_), custom_call_target="tpu_custom_call" | custom-call | flops 113246208 | bytes 1966080 | tf_op jit(solution)/shard_map/attention/pallas_call | solution.py:205
  87.4 3.2 %collective-permute-start.7 = (bf16[4,136,128]{2,1,0:T(8,128)(2,1)S(1)}, bf16[4,136,128]{2,1,0:T(8,128)(2,1)S(1)}, u32[]{:S(2)}, u32[]{:S(2)}) collective-permute-start(bf16[4,136,128]{2,1,0:T(8,128)(2,1)S(1)} %attention.8), channel_id=1, source_target_pairs={{58,0},{7,1},{60,2},{9,3},{62,4},{11,5},{0,6},{13,7},{2,8},{15,9},... | collective-permute-start | bytes 417800 | tf_op jit(solution)/shard_map/ppermute | solution.py:41
  90.6 1.8 %attention.7.refs_0_ = bf16[5,136,128]{2,1,0:T(8,128)(2,1)S(1)} custom-call(s32[258]{0:T(512)S(1)} %pad_add_fusion.1.refs_0_, bf16[5,144,128]{2,1,0:T(8,128)(2,1)S(1)} %get-tuple-element.42.refs_1_, bf16[5,384,512]{2,1,0:T(8,128)(2,1)S(1)} %get-tuple-element.43.refs_2_, bf16[5,384,128]{2,1,0:T(8,128)(2,1)S(1)} %get-tuple-element.44.refs_3_), custom_call_target="tpu_custom_call" | custom-call | flops 141557760 | bytes 2457600 | tf_op jit(solution)/shard_map/attention/pallas_call | solution.py:205
  92.4 2.5 %collective-permute-done.7.refs_1_ = bf16[4,136,128]{2,1,0:T(8,128)(2,1)S(1)} collective-permute-done((bf16[4,136,128]{2,1,0:T(8,128)(2,1)S(1)}, bf16[4,136,128]{2,1,0:T(8,128)(2,1)S(1)}, u32[]{:S(2)}, u32[]{:S(2)}) %collective-permute-start.7) | collective-permute-done | bytes 139296 | tf_op jit(solution)/shard_map/ppermute | solution.py:41
  94.9 1.6 %collective-permute-done.11.refs_3_ = bf16[5,136,128]{2,1,0:T(8,128)(2,1)S(1)} collective-permute-done((bf16[5,136,128]{2,1,0:T(8,128)(2,1)S(1)}, bf16[5,136,128]{2,1,0:T(8,128)(2,1)S(1)}, u32[]{:S(2)}, u32[]{:S(2)}) %collective-permute-start.11) | collective-permute-done | bytes 174112 | tf_op jit(solution)/shard_map/ppermute | solution.py:41
  96.9 6.0 %collective-permute-start.18 = (bf16[2,136,128]{2,1,0:T(8,128)(2,1)S(1)}, bf16[2,136,128]{2,1,0:T(8,128)(2,1)S(1)}, u32[]{:S(2)}, u32[]{:S(2)}) collective-permute-start(bf16[2,136,128]{2,1,0:T(8,128)(2,1)S(1)} %get-tuple-element.60), channel_id=1, source_target_pairs={{0,1},{1,0},{2,3},{3,2},{4,5},{5,4},{6,7},{7,6},{8,9},{9,8},{10,11... | collective-permute-start | bytes 208904 | tf_op jit(solution)/shard_map/ppermute | solution.py:46
  103.8 5.5 %collective-permute-start.19 = (bf16[2,136,128]{2,1,0:T(8,128)(2,1)S(1)}, bf16[2,136,128]{2,1,0:T(8,128)(2,1)S(1)}, u32[]{:S(2)}, u32[]{:S(2)}) collective-permute-start(bf16[2,136,128]{2,1,0:T(8,128)(2,1)S(1)} %get-tuple-element.61), channel_id=1, source_target_pairs={{52,0},{13,1},{54,2},{15,3},{56,4},{17,5},{58,6},{19,7},{60,8},{21... | collective-permute-start | bytes 208904 | tf_op jit(solution)/shard_map/ppermute | solution.py:41
  109.3 6.0 %collective-permute-start.20 = (bf16[2,136,128]{2,1,0:T(8,128)(2,1)S(1)}, bf16[2,136,128]{2,1,0:T(8,128)(2,1)S(1)}, u32[]{:S(2)}, u32[]{:S(2)}) collective-permute-start(bf16[2,136,128]{2,1,0:T(8,128)(2,1)S(1)} %get-tuple-element.62), channel_id=1, source_target_pairs={{38,0},{27,1},{40,2},{29,3},{42,4},{31,5},{44,6},{33,7},{46,8},{35... | collective-permute-start | bytes 208904 | tf_op jit(solution)/shard_map/ppermute | solution.py:41
  115.3 16.3 %collective-permute-done.20.refs_1_.refs_2_ = bf16[2,136,128]{2,1,0:T(8,128)(2,1)S(1)} collective-permute-done((bf16[2,136,128]{2,1,0:T(8,128)(2,1)S(1)}, bf16[2,136,128]{2,1,0:T(8,128)(2,1)S(1)}, u32[]{:S(2)}, u32[]{:S(2)}) %collective-permute-start.20) | collective-permute-done | bytes 69664 | tf_op jit(solution)/shard_map/ppermute | solution.py:41
  (57 shorter events, 18.4 us)
Async XLA Ops:
  1.0 0.8 copy-start
  1.7 21.3 %collective-permute-start = (bf16[1,144,128]{2,1,0:T(8,128)(2,1)S(1)}, bf16[1,144,128]{2,1,0:T(8,128)(2,1)S(1)}, u32[]{:S(2)}, u32[]{:S(2)}) collective-permute-start(bf16[1,144,128]{2,1,0:T(8,128)(2,1)S(1)} %pack.1.refs_0_), channel_id=1, source_target_pairs={{0,1},{1,0},{2,3},{3,2},{4,5},{5,4},{6,7},{7,6},{8,9},{9,8},{10,11... | collective-permute-start | bytes 110600 | tf_op jit(solution)/shard_map/ppermute | solution.py:46
  23.0 18.7 %collective-permute-start.4 = (bf16[96,64,512]{2,1,0:T(8,128)(2,1)}, bf16[96,64,512]{2,1,0:T(8,128)(2,1)}, u32[]{:S(2)}, u32[]{:S(2)}) collective-permute-start(bf16[96,64,512]{2,1,0:T(8,128)(2,1)} %refs_1_.1), channel_id=1, source_target_pairs={{0,1},{1,0},{2,3},{3,2},{4,5},{5,4},{6,7},{7,6},{8,9},{9,8},{10,11... | collective-permute-start | bytes 18874376 | tf_op jit(solution)/shard_map/ppermute | solution.py:46
  23.4 13.5 %collective-permute-start.1 = (bf16[96,4096]{1,0:T(8,128)(2,1)}, bf16[96,4096]{1,0:T(8,128)(2,1)S(1)}, u32[]{:S(2)}, u32[]{:S(2)}) collective-permute-start(bf16[96,4096]{1,0:T(8,128)(2,1)} %param.9), channel_id=1, source_target_pairs={{0,1},{1,0},{2,3},{3,2},{4,5},{5,4},{6,7},{7,6},{8,9},{9,8},{10,11... | collective-permute-start | bytes 2359304 | tf_op jit(solution)/shard_map/ppermute | solution.py:46
  23.5 25.2 %collective-permute-start.2 = (bf16[2,144,128]{2,1,0:T(8,128)(2,1)S(1)}, bf16[2,144,128]{2,1,0:T(8,128)(2,1)S(1)}, u32[]{:S(2)}, u32[]{:S(2)}) collective-permute-start(bf16[2,144,128]{2,1,0:T(8,128)(2,1)S(1)} %shard_map.64), channel_id=1, source_target_pairs={{12,0},{53,1},{14,2},{55,3},{16,4},{57,5},{18,6},{59,7},{20,8},{61... | collective-permute-start | bytes 221192 | tf_op jit(solution)/shard_map/ppermute | solution.py:41
  23.5 25.8 %collective-permute-start.3 = (bf16[2,144,128]{2,1,0:T(8,128)(2,1)S(1)}, bf16[2,144,128]{2,1,0:T(8,128)(2,1)S(1)}, u32[]{:S(2)}, u32[]{:S(2)}) collective-permute-start(bf16[2,144,128]{2,1,0:T(8,128)(2,1)S(1)} %shard_map.64), channel_id=1, source_target_pairs={{26,0},{39,1},{28,2},{41,3},{30,4},{43,5},{32,6},{45,7},{34,8},{47... | collective-permute-start | bytes 221192 | tf_op jit(solution)/shard_map/ppermute | solution.py:41
  49.4 4.4 %collective-permute-start.5 = (bf16[2,144,128]{2,1,0:T(8,128)(2,1)S(1)}, bf16[2,144,128]{2,1,0:T(8,128)(2,1)S(1)}, u32[]{:S(2)}, u32[]{:S(2)}) collective-permute-start(bf16[2,144,128]{2,1,0:T(8,128)(2,1)S(1)} %shard_map.65), channel_id=1, source_target_pairs={{0,1},{1,0},{2,3},{3,2},{4,5},{5,4},{6,7},{7,6},{8,9},{9,8},{10,11... | collective-permute-start | bytes 221192 | tf_op jit(solution)/shard_map/ppermute | solution.py:46
  53.9 8.9 %collective-permute-start.8 = (bf16[3,144,128]{2,1,0:T(8,128)(2,1)S(1)}, bf16[3,144,128]{2,1,0:T(8,128)(2,1)S(1)}, u32[]{:S(2)}, u32[]{:S(2)}) collective-permute-start(bf16[3,144,128]{2,1,0:T(8,128)(2,1)S(1)} %get-tuple-element.48), channel_id=1, source_target_pairs={{58,0},{7,1},{60,2},{9,3},{62,4},{11,5},{0,6},{13,7},{2,8},{15,9},... | collective-permute-start | bytes 331784 | tf_op jit(solution)/shard_map/ppermute | solution.py:41
  58.5 12.4 %collective-permute-start.16 = (bf16[5,144,128]{2,1,0:T(8,128)(2,1)S(1)}, bf16[5,144,128]{2,1,0:T(8,128)(2,1)S(1)}, u32[]{:S(2)}, u32[]{:S(2)}) collective-permute-start(bf16[5,144,128]{2,1,0:T(8,128)(2,1)S(1)} %get-tuple-element.42.refs_1_), channel_id=1, source_target_pairs={{62,0},{3,1},{0,2},{5,3},{2,4},{7,5},{4,6},{9,7},{6,8},{11,9},{8,1... | collective-permute-start | bytes 552968 | tf_op jit(solution)/shard_map/ppermute | solution.py:41
  58.5 15.3 %collective-permute-start.14 = (bf16[5,144,128]{2,1,0:T(8,128)(2,1)S(1)}, bf16[5,144,128]{2,1,0:T(8,128)(2,1)S(1)}, u32[]{:S(2)}, u32[]{:S(2)}) collective-permute-start(bf16[5,144,128]{2,1,0:T(8,128)(2,1)S(1)} %get-tuple-element.42.refs_1_), channel_id=1, source_target_pairs={{2,0},{63,1},{4,2},{1,3},{6,4},{3,5},{8,6},{5,7},{10,8},{7,9},{12,... | collective-permute-start | bytes 552968 | tf_op jit(solution)/shard_map/ppermute | solution.py:41
  59.9 17.8 %collective-permute-start.12 = (bf16[5,144,128]{2,1,0:T(8,128)(2,1)S(1)}, bf16[5,144,128]{2,1,0:T(8,128)(2,1)S(1)}, u32[]{:S(2)}, u32[]{:S(2)}) collective-permute-start(bf16[5,144,128]{2,1,0:T(8,128)(2,1)S(1)} %get-tuple-element.42.refs_1_), channel_id=1, source_target_pairs={{60,0},{5,1},{62,2},{7,3},{0,4},{9,5},{2,6},{11,7},{4,8},{13,9},{6... | collective-permute-start | bytes 552968 | tf_op jit(solution)/shard_map/ppermute | solution.py:41
  59.9 20.3 %collective-permute-start.10 = (bf16[5,144,128]{2,1,0:T(8,128)(2,1)S(1)}, bf16[5,144,128]{2,1,0:T(8,128)(2,1)S(1)}, u32[]{:S(2)}, u32[]{:S(2)}) collective-permute-start(bf16[5,144,128]{2,1,0:T(8,128)(2,1)S(1)} %get-tuple-element.42.refs_1_), channel_id=1, source_target_pairs={{4,0},{61,1},{6,2},{63,3},{8,4},{1,5},{10,6},{3,7},{12,8},{5,9},{1... | collective-permute-start | bytes 552968 | tf_op jit(solution)/shard_map/ppermute | solution.py:41
  62.8 21.8 %collective-permute-start.6 = (bf16[4,144,128]{2,1,0:T(8,128)(2,1)S(1)}, bf16[4,144,128]{2,1,0:T(8,128)(2,1)S(1)}, u32[]{:S(2)}, u32[]{:S(2)}) collective-permute-start(bf16[4,144,128]{2,1,0:T(8,128)(2,1)S(1)} %get-tuple-element.45), channel_id=1, source_target_pairs={{6,0},{59,1},{8,2},{61,3},{10,4},{63,5},{12,6},{1,7},{14,8},{3,9},... | collective-permute-start | bytes 442376 | tf_op jit(solution)/shard_map/ppermute | solution.py:41
  70.9 16.6 %collective-permute-start.9 = (bf16[3,136,128]{2,1,0:T(8,128)(2,1)S(1)}, bf16[3,136,128]{2,1,0:T(8,128)(2,1)S(1)}, u32[]{:S(2)}, u32[]{:S(2)}) collective-permute-start(bf16[3,136,128]{2,1,0:T(8,128)(2,1)S(1)} %attention.9), channel_id=1, source_target_pairs={{6,0},{59,1},{8,2},{61,3},{10,4},{63,5},{12,6},{1,7},{14,8},{3,9},... | collective-permute-start | bytes 313352 | tf_op jit(solution)/shard_map/ppermute | solution.py:41
  73.8 21.1 %collective-permute-start.17 = (bf16[5,136,128]{2,1,0:T(8,128)(2,1)S(1)}, bf16[5,136,128]{2,1,0:T(8,128)(2,1)S(1)}, u32[]{:S(2)}, u32[]{:S(2)}) collective-permute-start(bf16[5,136,128]{2,1,0:T(8,128)(2,1)S(1)} %attention.13), channel_id=1, source_target_pairs={{2,0},{63,1},{4,2},{1,3},{6,4},{3,5},{8,6},{5,7},{10,8},{7,9},{12,... | collective-permute-start | bytes 522248 | tf_op jit(solution)/shard_map/ppermute | solution.py:41
  77.7 17.2 %collective-permute-start.15 = (bf16[5,136,128]{2,1,0:T(8,128)(2,1)S(1)}, bf16[5,136,128]{2,1,0:T(8,128)(2,1)S(1)}, u32[]{:S(2)}, u32[]{:S(2)}) collective-permute-start(bf16[5,136,128]{2,1,0:T(8,128)(2,1)S(1)} %attention.12), channel_id=1, source_target_pairs={{62,0},{3,1},{0,2},{5,3},{2,4},{7,5},{4,6},{9,7},{6,8},{11,9},{8,1... | collective-permute-start | bytes 522248 | tf_op jit(solution)/shard_map/ppermute | solution.py:41
  80.2 14.7 %collective-permute-start.13 = (bf16[5,136,128]{2,1,0:T(8,128)(2,1)S(1)}, bf16[5,136,128]{2,1,0:T(8,128)(2,1)S(1)}, u32[]{:S(2)}, u32[]{:S(2)}) collective-permute-start(bf16[5,136,128]{2,1,0:T(8,128)(2,1)S(1)} %attention.11), channel_id=1, source_target_pairs={{4,0},{61,1},{6,2},{63,3},{8,4},{1,5},{10,6},{3,7},{12,8},{5,9},{1... | collective-permute-start | bytes 522248 | tf_op jit(solution)/shard_map/ppermute | solution.py:41
  84.6 11.9 %collective-permute-start.11 = (bf16[5,136,128]{2,1,0:T(8,128)(2,1)S(1)}, bf16[5,136,128]{2,1,0:T(8,128)(2,1)S(1)}, u32[]{:S(2)}, u32[]{:S(2)}) collective-permute-start(bf16[5,136,128]{2,1,0:T(8,128)(2,1)S(1)} %attention.10), channel_id=1, source_target_pairs={{60,0},{5,1},{62,2},{7,3},{0,4},{9,5},{2,6},{11,7},{4,8},{13,9},{6... | collective-permute-start | bytes 522248 | tf_op jit(solution)/shard_map/ppermute | solution.py:41
  87.4 7.5 %collective-permute-start.7 = (bf16[4,136,128]{2,1,0:T(8,128)(2,1)S(1)}, bf16[4,136,128]{2,1,0:T(8,128)(2,1)S(1)}, u32[]{:S(2)}, u32[]{:S(2)}) collective-permute-start(bf16[4,136,128]{2,1,0:T(8,128)(2,1)S(1)} %attention.8), channel_id=1, source_target_pairs={{58,0},{7,1},{60,2},{9,3},{62,4},{11,5},{0,6},{13,7},{2,8},{15,9},... | collective-permute-start | bytes 417800 | tf_op jit(solution)/shard_map/ppermute | solution.py:41
  96.9 6.9 %collective-permute-start.18 = (bf16[2,136,128]{2,1,0:T(8,128)(2,1)S(1)}, bf16[2,136,128]{2,1,0:T(8,128)(2,1)S(1)}, u32[]{:S(2)}, u32[]{:S(2)}) collective-permute-start(bf16[2,136,128]{2,1,0:T(8,128)(2,1)S(1)} %get-tuple-element.60), channel_id=1, source_target_pairs={{0,1},{1,0},{2,3},{3,2},{4,5},{5,4},{6,7},{7,6},{8,9},{9,8},{10,11... | collective-permute-start | bytes 208904 | tf_op jit(solution)/shard_map/ppermute | solution.py:46
  103.8 11.5 %collective-permute-start.19 = (bf16[2,136,128]{2,1,0:T(8,128)(2,1)S(1)}, bf16[2,136,128]{2,1,0:T(8,128)(2,1)S(1)}, u32[]{:S(2)}, u32[]{:S(2)}) collective-permute-start(bf16[2,136,128]{2,1,0:T(8,128)(2,1)S(1)} %get-tuple-element.61), channel_id=1, source_target_pairs={{52,0},{13,1},{54,2},{15,3},{56,4},{17,5},{58,6},{19,7},{60,8},{21... | collective-permute-start | bytes 208904 | tf_op jit(solution)/shard_map/ppermute | solution.py:41
  109.3 22.3 %collective-permute-start.20 = (bf16[2,136,128]{2,1,0:T(8,128)(2,1)S(1)}, bf16[2,136,128]{2,1,0:T(8,128)(2,1)S(1)}, u32[]{:S(2)}, u32[]{:S(2)}) collective-permute-start(bf16[2,136,128]{2,1,0:T(8,128)(2,1)S(1)} %get-tuple-element.62), channel_id=1, source_target_pairs={{38,0},{27,1},{40,2},{29,3},{42,4},{31,5},{44,6},{33,7},{46,8},{35... | collective-permute-start | bytes 208904 | tf_op jit(solution)/shard_map/ppermute | solution.py:41
  131.7 1.3 collective-permute-start.21
